TPU v7x, 128 devices: a whole 4x4x4 slice. The times are simulated.
128 devices in a mesh: seq: 32 (over x, z, core), tp: 4 (over y).
Axes of the slice: x: 4, y: 4, z: 4, core: 2. Of those that a mesh axis runs over, the one named last changes fastest.
Arguments:
- tokens: bfloat16 [65536, 2560], P('seq'), may hold values from -6 to 6
- w_query: bfloat16 [2560, 512], P(None, 'tp'), may hold values from -0.009765625 to 0.009765625
- w_key: bfloat16 [2560, 512], P(None, 'tp'), may hold values from -0.00048828125 to 0.00048828125
- w_value: bfloat16 [2560, 1024], P(None, 'tp'), may hold values from -0.125 to 0.125
- w_gate: bfloat16 [2560, 512], P(None, 'tp'), may hold values from -0.125 to 0.125
- gate_rate: float32 [512], P('tp'), may hold values from 3.8146973e-06 to 3.0517578e-05
- out_grad: bfloat16 [65536, 1024], P('seq', 'tp'), may hold values from -6 to 6
Outputs:
- input_grad: bfloat16 [65536, 2560], P(('seq', 'tp'))
- gate_signal: float32 [65536, 512], P('seq', 'tp')
All inputs are finite; a program needn't handle non-finite values.
Results may differ from a plain program's by a relative error of at most 0.015.
Values sent between devices are 32-bit elements.
A program may use at most 192 MiB of HBM per device.

v0:
```python
import math

import jax
import jax.numpy as jnp
from jax import lax
from jax.sharding import Mesh
from jax.sharding import PartitionSpec as P

DK = 128
DV = 256
CH = 128
SEQ = ("seq_0", "seq_1", "seq_2")
SEQ_TP = ("seq_0", "seq_1", "seq_2", "tp")


def neutral_like(x, identity):
    return jax.tree.map(
        lambda part, zero: jnp.zeros_like(part) + jnp.asarray(zero, part.dtype), x, identity
    )


def carried_in(x, axes, combine, identity, reverse):
    before = start = neutral_like(x, identity)
    so_far = x
    for axis in reversed(axes):
        devices, position = lax.axis_size(axis), lax.axis_index(axis)
        pieces = jax.tree.map(lambda part: lax.all_gather(part, axis), so_far)
        inside, so_far = start, start
        for k in reversed(range(devices)) if reverse else range(devices):
            passed = k > position if reverse else k < position
            so_far = combine(so_far, jax.tree.map(lambda part: part[k], pieces))
            inside = jax.tree.map(lambda new, old: jnp.where(passed, new, old), so_far, inside)
        before = combine(inside, before)
    return before


def lower_ones(length):
    places = jnp.arange(length)
    return (places[:, None] >= places[None, :]).astype(jnp.float32)


def low_dot(left, right):
    return jnp.dot(
        left.astype(jnp.bfloat16), right.astype(jnp.bfloat16), preferred_element_type=jnp.float32
    )


def run_head(query_rows, key_rows, value_rows, log_gate, initial):
    block_size = CH
    blocks_count = query_rows.shape[0] // block_size
    triangle = lower_ones(block_size)
    pieces = tuple(
        (
            a.reshape(blocks_count, block_size, a.shape[1])
            for a in (query_rows, key_rows, value_rows, log_gate)
        )
    )

    def advance(memory, piece):
        query_block, key_block, value_block, gate_block = piece
        within = jnp.cumsum(gate_block, axis=0)
        closing = within[-1]
        query_scaled = query_block * jnp.exp(within)
        key_scaled = key_block * jnp.exp(-within)
        scores = low_dot(query_scaled, key_scaled.T) * triangle
        output = low_dot(query_scaled, memory) + low_dot(scores, value_block)
        key_closing = key_block * jnp.exp(closing - within)
        memory = jnp.exp(closing)[:, None] * memory + low_dot(key_closing.T, value_block)
        return (memory, output)

    last_memory, outputs = lax.scan(advance, initial, pieces)
    return (outputs.reshape(-1, outputs.shape[2]), last_memory)


def by_heads(matrix, width):
    return matrix.astype(jnp.float32).reshape(matrix.shape[0], -1, width).transpose(1, 0, 2)


def by_tokens(stacked):
    return stacked.transpose(1, 0, 2).reshape(stacked.shape[1], -1)


def back_project(grad_rows, weight):
    return lax.dot_general(
        grad_rows, weight, (((1,), (1,)), ((), ())), preferred_element_type=jnp.float32
    )


def compose(earlier, later):
    return (later[0] * earlier[0], later[0][..., None] * earlier[1] + later[1])


def per_device(tokens, w_query, w_key, w_value, w_gate, gate_rate, out_grad):
    queries = jnp.dot(tokens, w_query, preferred_element_type=jnp.float32).astype(jnp.bfloat16)
    keys_proj = jnp.dot(tokens, w_key, preferred_element_type=jnp.float32).astype(jnp.bfloat16)
    values_proj = jnp.dot(tokens, w_value, preferred_element_type=jnp.float32).astype(jnp.bfloat16)
    squashed = jax.nn.sigmoid(jnp.dot(tokens, w_gate, preferred_element_type=jnp.float32))
    log_gate = -gate_rate * squashed
    query_heads = by_heads(queries, DK)
    key_heads = by_heads(keys_proj, DK)
    value_heads = by_heads(values_proj, DV)
    gate_heads = by_heads(log_gate, DK)
    grad_heads = by_heads(out_grad, DV)
    running = jnp.cumsum(log_gate, axis=0)
    total = running[-1]
    decay = jnp.exp(total).reshape(-1, DK)
    fed_keys = (keys_proj.astype(jnp.float32) * jnp.exp(total - running)).astype(jnp.bfloat16)
    fed_keys = fed_keys.reshape(fed_keys.shape[0], -1, DK)
    local_state = jnp.einsum(
        "lhd,lhe->hde",
        fed_keys,
        values_proj.reshape(values_proj.shape[0], -1, DV),
        preferred_element_type=jnp.float32,
    )
    fed_queries = (queries.astype(jnp.float32) * jnp.exp(running)).astype(jnp.bfloat16)
    fed_queries = fed_queries.reshape(fed_queries.shape[0], -1, DK)
    local_cotangent = jnp.einsum(
        "lhd,lhe->hde",
        fed_queries,
        out_grad.reshape(out_grad.shape[0], -1, DV),
        preferred_element_type=jnp.float32,
    )
    zero_state = jnp.zeros_like(local_state)
    identity = (jnp.ones_like(decay), zero_state)
    start_state = carried_in((decay, local_state), SEQ, compose, identity, False)[1]
    end_grad = carried_in((decay, local_cotangent), SEQ, compose, identity, True)[1]

    def local_run(query_part, key_part, value_part, gate_part):
        return jax.vmap(run_head)(query_part, key_part, value_part, gate_part, start_state)

    unused_outputs, pullback = jax.vjp(local_run, query_heads, key_heads, value_heads, gate_heads)
    grads = pullback((grad_heads, end_grad))
    query_grad = by_tokens(grads[0]).astype(jnp.bfloat16)
    key_grad = by_tokens(grads[1]).astype(jnp.bfloat16)
    value_grad = by_tokens(grads[2]).astype(jnp.bfloat16)
    pre_grad = by_tokens(grads[3]) * -gate_rate * squashed * (1.0 - squashed)
    whole_tokens = tokens.shape[0] * lax.axis_size(SEQ)
    gate_signal = pre_grad * (4.0 * math.sqrt(whole_tokens * DK / DV))
    gate_grad = pre_grad.astype(jnp.bfloat16)

    def term(rows_count):

        def rows_of(matrix):
            return lax.slice_in_dim(matrix, 0, rows_count, axis=0)

        mixed = back_project(rows_of(query_grad), w_query) + back_project(rows_of(key_grad), w_key)
        return (
            mixed
            + back_project(rows_of(value_grad), w_value)
            + back_project(rows_of(gate_grad), w_gate)
        )

    summed = lax.psum_scatter(
        term(tokens.shape[0] // lax.axis_size("tp") * lax.axis_size("tp")),
        "tp",
        scatter_dimension=0,
        tiled=True,
    )
    return (summed.astype(jnp.bfloat16), gate_signal)


def solution(mesh):
    torus = Mesh(mesh.devices.reshape(4, 4, 2, mesh.shape["tp"]), ("seq_0", "seq_1", "seq_2", "tp"))
    placed = (
        P(SEQ, None),
        P(None, "tp"),
        P(None, "tp"),
        P(None, "tp"),
        P(None, "tp"),
        P("tp"),
        P(SEQ, "tp"),
    )
    return jax.shard_map(
        per_device,
        mesh=torus,
        in_specs=placed,
        out_specs=(P(SEQ_TP, None), P(SEQ, "tp")),
        check_vma=False,
    )
```

profile of v0, /device:TPU:1, one launch (start us, length us, event | category | flops | bytes accessed | tf_op | source)
XLA Modules:
  0.0 726.5 jit_solution(12167992358769536140)
XLA Ops:
  9.3 8.1 %fusion.89 = f32[2048,128]{1,0:T(8,128)} fusion(bf16[2048,2560]{1,0:T(8,128)(2,1)} %param.11, bf16[2560,128]{1,0:T(8,128)(2,1)} %param.12), kind=kOutput, calls=%fused_computation.137 | convolution fusion | flops 1342701568 | bytes 12189696 | tf_op jit(solution)/shard_map/dot_general | solution.py:94
  17.4 3.9 fusion.88
  21.3 3.9 convolution_convert_fusion.8
  25.1 3.9 broadcast_multiply_fusion
  31.1 2.8 all-gather.4
  33.9 9.1 %all-gather.5 = f32[4,1,128]{2,1,0:T(1,128)S(1)} all-gather(f32[1,1,128]{2,1,0:T(1,128)S(1)} %get-tuple-element.952), channel_id=5, replica_groups=mesh['seq_0'=4,'seq_1'=4,'seq_2'=2,'tp'=4] {'seq_1'}, dimensions={0}, use_global_device_ids=true | all-gather | bytes 2560 | tf_op jit(solution)/shard_map/all_gather | solution.py:27
  43.1 7.7 %all_gather.53 = f32[4,1,128]{2,1,0:T(1,128)S(1)} all-gather(f32[1,1,128]{2,1,0:T(1,128)S(1)} %get-tuple-element.934), channel_id=1, replica_groups=mesh['seq_0'=4,'seq_1'=4,'seq_2'=2,'tp'=4] {'seq_0'}, dimensions={0}, use_global_device_ids=true | all-gather | bytes 2560 | tf_op jit(solution)/shard_map/all_gather | solution.py:27
  50.8 5.2 all_gather.48
  57.7 7.9 %all-gather.1 = f32[256,256]{1,0:T(8,128)S(1)} all-gather(f32[128,256]{1,0:T(8,128)S(1)} %fusion.94), channel_id=3, replica_groups=mesh['seq_0'=4,'seq_1'=4,'seq_2'=2,'tp'=4] {'seq_2'}, dimensions={0}, use_global_device_ids=true | all-gather | bytes 393216 | tf_op jit(solution)/shard_map/all_gather | solution.py:27
  65.6 2.0 fusion.95
  67.6 2.0 all-gather.2
  69.7 9.9 %all_gather.51 = f32[4,1,128,256]{3,2,1,0:T(8,128)S(1)} all-gather(f32[1,1,128,256]{3,2,1,0:T(8,128)S(1)} %bitcast_add_fusion.17), channel_id=1, replica_groups=mesh['seq_0'=4,'seq_1'=4,'seq_2'=2,'tp'=4] {'seq_1'}, dimensions={0}, use_global_device_ids=true | all-gather | bytes 655360 | tf_op jit(solution)/shard_map/all_gather | solution.py:27
  79.7 11.0 %all_gather.56 = f32[4,1,128,256]{3,2,1,0:T(8,128)S(1)} all-gather(f32[1,1,128,256]{3,2,1,0:T(8,128)S(1)} %bitcast_add_fusion.9), channel_id=1, replica_groups=mesh['seq_0'=4,'seq_1'=4,'seq_2'=2,'tp'=4] {'seq_1'}, dimensions={0}, use_global_device_ids=true | all-gather | bytes 655360 | tf_op jit(solution)/shard_map/all_gather | solution.py:27
  91.6 10.0 %all_gather.57 = f32[4,1,128,256]{3,2,1,0:T(8,128)S(1)} all-gather(f32[1,1,128,256]{3,2,1,0:T(8,128)S(1)} %get-tuple-element.948), channel_id=1, replica_groups=mesh['seq_0'=4,'seq_1'=4,'seq_2'=2,'tp'=4] {'seq_0'}, dimensions={0}, use_global_device_ids=true | all-gather | bytes 655360 | tf_op jit(solution)/shard_map/all_gather | solution.py:27
  105.2 138.9 %while.64 = (s32[]{:T(128)}, f32[1,128,256]{2,1,0:T(8,128)S(1)}, f32[16,1,128,128]{3,2,1,0:T(8,128)}, f32[16,1,128,128]{3,2,1,0:T(8,128)}, bf16[16,1,128,128]{2,...) while((s32[]{:T(128)}, f32[1,128,256]{2,1,0:T(8,128)S(1)}, ...), condition=%wide.region_4.5_spmd.clone.clone, body=%wide.region_2.4_spmd.clone.sunk.clone | while | flops 14991362 | bytes 2036953 | solution.py:71
  244.2 10.1 %all_gather.52 = f32[4,1,128,256]{3,2,1,0:T(8,128)S(1)} all-gather(f32[1,1,128,256]{3,2,1,0:T(8,128)} %get-tuple-element.949), channel_id=1, replica_groups=mesh['seq_0'=4,'seq_1'=4,'seq_2'=2,'tp'=4] {'seq_0'}, dimensions={0}, use_global_device_ids=true | all-gather | bytes 655360 | tf_op jit(solution)/shard_map/all_gather | solution.py:27
  256.9 210.4 %while.65 = (s32[]{:T(128)}, f32[1,128,256]{1,2,0:T(8,128)S(1)}, bf16[16,1,128,128]{3,2,1,0:T(8,128)(2,1)}, bf16[16,1,128,128]{3,2,1,0:T(8,128)(2,1)S(1)}, bf16[...) while((s32[]{:T(128)}, f32[1,128,256]{1,2,0:T(8,128)S(1)}, ...), condition=%wide.region_9.10_spmd.clone.clone, body=%wide.region_5.9_spmd.clone.sunk.clone | while | flops 61521920 | bytes 4141797 | solution.py:71
  433.9 1.6 bitcast_dynamic-update-slice_fusion.19
  467.3 10.0 %fusion.138 = f32[2048,2560]{1,0:T(8,128)} fusion(bf16[2048,256]{1,0:T(8,128)(2,1)} %bitcast.677, bf16[2560,256]{1,0:T(8,128)(2,1)S(1)} %copy-done), kind=kOutput, calls=%fused_computation.248 | convolution fusion | flops 2684354560 | bytes 23330816 | tf_op jit(solution)/shard_map/dot_general | solution.py:84
  477.3 8.6 %fusion.136 = f32[2048,2560]{1,0:T(8,128)} fusion(bf16[2048,128]{1,0:T(8,128)(2,1)S(1)} %bitcast.675, bf16[2560,128]{1,0:T(8,128)(2,1)S(1)} %copy-done.12), kind=kOutput, calls=%fused_computation.246 | convolution fusion | flops 1342177280 | bytes 22151168 | tf_op jit(solution)/shard_map/dot_general | solution.py:84
  485.9 8.7 %fusion.137 = f32[2048,2560]{1,0:T(8,128)} fusion(bf16[2048,128]{1,0:T(8,128)(2,1)S(1)} %bitcast.676, bf16[2560,128]{1,0:T(8,128)(2,1)S(1)} %copy-done.14), kind=kOutput, calls=%fused_computation.247 | convolution fusion | flops 1342177280 | bytes 22151168 | tf_op jit(solution)/shard_map/dot_general | solution.py:84
  495.8 28.3 %add_add_fusion = f32[2048,2560]{1,0:T(8,128)} fusion(f32[2048,2560]{1,0:T(8,128)} %fusion.138, f32[2048,2560]{1,0:T(8,128)} %fusion.136, f32[2048,2560]{1,0:T(8,128)} %fusion.137, bf16[2560,128]{1,0:T(8,128)(2,1)} %param.15, bf16[2048,128]{1,0:T(8,128)(2,1)S(1)} %get-tuple-element.906), kind=kOutput, calls=%fused_computation.128 | convolution fusion | flops 1357905920 | bytes 85065728 | tf_op jit(solution)/shard_map/dot_general | solution.py:84
  524.2 191.3 %reduce-scatter.2.cloned.1.call-done = f32[512,2560]{1,0:T(8,128)} async-done(((f32[2048,2560]{1,0:T(8,128)}), f32[512,2560]{1,0:T(8,128)}) %reduce-scatter.2.cloned.1.call-update) | async-done | bytes 5242896 | tf_op jit(solution)/shard_map/reduce_scatter | solution.py:153
  715.4 4.3 convert_element_type.319
  (520 shorter events, 361.0 us)
Async XLA Ops:
  7.2 14.1 %copy-start = (bf16[2560,256]{1,0:T(8,128)(2,1)S(1)}, bf16[2560,256]{1,0:T(8,128)(2,1)}, u32[]{:S(2)}) copy-start(bf16[2560,256]{1,0:T(8,128)(2,1)} %param.14) | copy-start | bytes 3932164
  7.2 10.2 %copy-start.13 = (bf16[2560,128]{1,0:T(8,128)(2,1)S(1)}, bf16[2560,128]{1,0:T(8,128)(2,1)}, u32[]{:S(2)}) copy-start(bf16[2560,128]{1,0:T(8,128)(2,1)} %param.13) | copy-start | bytes 1966084
  7.2 708.2 %reduce-scatter.2.cloned.1.call-start = ((), (), s32[]{:S(2)}) async-start(), calls=%async_computation.1 | async-start | bytes 26214400 | tf_op jit(solution)/shard_map/reduce_scatter | solution.py:153
  7.4 13.9 %copy-start.3 = (bf16[16,1,128,128]{3,2,1,0:T(8,128)(2,1)}, bf16[16,1,128,128]{3,2,1,0:T(8,128)(2,1)S(1)}, u32[]{:S(2)}) copy-start(bf16[16,1,128,128]{3,2,1,0:T(8,128)(2,1)S(1)} %fusion.131) | copy-start | bytes 1572868
  8.5 8.9 %copy-start.16 = (bf16[2048,2560]{1,0:T(8,128)(2,1)S(1)}, bf16[2048,2560]{1,0:T(8,128)(2,1)}, u32[]{:S(2)}) copy-start(bf16[2048,2560]{1,0:T(8,128)(2,1)} %param.11) | copy-start | bytes 31457284
  21.3 3.9 copy-start.15
  25.1 30.9 %copy-start.2 = (bf16[2048,256]{1,0:T(8,128)(2,1)S(1)}, bf16[2048,256]{1,0:T(8,128)(2,1)}, u32[]{:S(2)}) copy-start(bf16[2048,256]{1,0:T(8,128)(2,1)} %param.17) | copy-start | bytes 3145732
  29.0 1.0 copy-start.10
  65.6 36.3 %copy-start.8 = (f32[256,256]{1,0:T(8,128)}, f32[256,256]{1,0:T(8,128)S(1)}, u32[]{:S(2)}) copy-start(f32[256,256]{1,0:T(8,128)S(1)} %all-gather.1) | copy-start | bytes 786436
  79.6 21.9 %copy-start.6 = (f32[4,1,128,256]{3,2,1,0:T(8,128)}, f32[4,1,128,256]{3,2,1,0:T(8,128)S(1)}, u32[]{:S(2)}) copy-start(f32[4,1,128,256]{3,2,1,0:T(8,128)S(1)} %all_gather.51) | copy-start | bytes 1572868
  90.8 166.1 %copy-start.5 = (bf16[16,1,128,128]{3,2,1,0:T(8,128)(2,1)S(1)}, bf16[16,1,128,128]{3,2,1,0:T(8,128)(2,1)}, u32[]{:S(2)}) copy-start(bf16[16,1,128,128]{3,2,1,0:T(8,128)(2,1)} %copy-done.3) | copy-start | bytes 1572868
  101.9 152.4 %copy-start.9 = (f32[256,256]{1,0:T(8,128)S(1)}, f32[256,256]{1,0:T(8,128)}, u32[]{:S(2)}) copy-start(f32[256,256]{1,0:T(8,128)} %copy-done.8) | copy-start | bytes 786436
  467.3 10.0 %copy-start.4 = (bf16[16,1,128,128]{3,2,1,0:T(8,128)(2,1)S(1)}, bf16[16,1,128,128]{3,2,1,0:T(8,128)(2,1)}, u32[]{:S(2)}) copy-start(bf16[16,1,128,128]{3,2,1,0:T(8,128)(2,1)} %get-tuple-element.657) | copy-start | bytes 1572868
  467.3 10.0 %copy-start.12 = (bf16[2560,128]{1,0:T(8,128)(2,1)S(1)}, bf16[2560,128]{1,0:T(8,128)(2,1)}, u32[]{:S(2)}) copy-start(bf16[2560,128]{1,0:T(8,128)(2,1)} %param.12) | copy-start | bytes 1966084
  477.3 8.6 %copy-start.14 = (bf16[2560,128]{1,0:T(8,128)(2,1)S(1)}, bf16[2560,128]{1,0:T(8,128)(2,1)}, u32[]{:S(2)}) copy-start(bf16[2560,128]{1,0:T(8,128)(2,1)} %param.13) | copy-start | bytes 1966084
  485.9 8.7 %copy-start.7 = (f32[16,1,128,128]{3,2,1,0:T(8,128)S(1)}, f32[16,1,128,128]{3,2,1,0:T(8,128)}, u32[]{:S(2)}) copy-start(f32[16,1,128,128]{3,2,1,0:T(8,128)} %get-tuple-element.660) | copy-start | bytes 3145732
  485.9 8.7 %copy-start.11 = (f32[2048,128]{1,0:T(8,128)S(1)}, f32[2048,128]{1,0:T(8,128)}, u32[]{:S(2)}) copy-start(f32[2048,128]{1,0:T(8,128)} %get-tuple-element.954) | copy-start | bytes 3145732
  524.1 195.5 %copy-start.1 = (bf16[2560,256]{1,0:T(8,128)(2,1)S(1)}, bf16[2560,256]{1,0:T(8,128)(2,1)}, u32[]{:S(2)}) copy-start(bf16[2560,256]{1,0:T(8,128)(2,1)} %param.14) | copy-start | bytes 3932164
Sparse Core Ops, SparseCore 0:
  524.3 191.0 reduce-scatter.1
where the time goes:
time: 739 us; the launch traced here: 727 us
  matrix products  256 us (35%)
  waiting for transfers between devices  191 us (26%)
  other arithmetic  131 us (18%)
  blocking collectives  75.9 us (10%)
  local copies, waits for them, and re-layouts  56.9 us (8%)
  between operations  14.3 us (2%)
    reduce_scatter x1, waiting for transfers between devices, per_device(): lax.psum_scatter(term(tokens.shape[0] // lax.axis_size('tp') * lax.axis_s...  191 us
    dot_general x160, matrix products, low_dot(): jnp.dot(left.astype(jnp.bfloat16), right.astype(jnp.bfloat16), preferred_...  177 us
    dynamic_update_slice x64, other arithmetic, run_head(): last_memory, outputs = lax.scan(advance, initial, pieces)  82.4 us
    all_gather x10, blocking collectives, carried_in(): pieces = jax.tree.map(lambda part: lax.all_gather(part, axis), so_far)  75.9 us
    dot_general x4, matrix products, back_project(): lax.dot_general(grad_rows, weight, (((1,), (1,)), ((), ())), preferred_el...  55.6 us
    another operation x48, other arithmetic, advance(): within = jnp.cumsum(gate_block, axis=0)  36.8 us
    dynamic_update_slice x64, local copies, waits for them, and re-layouts, run_head(): last_memory, outputs = lax.scan(advance, initial, pieces)  21.2 us
    dynamic_slice x32, local copies, waits for them, and re-layouts, run_head(): last_memory, outputs = lax.scan(advance, initial, pieces)  16.1 us
  transfers between devices with their start and end apart: 1, of which 1 were waited for; matrix products, arithmetic and copies ran while one was open for 0% of the time, Pallas kernels for 0%

commit v1 on v0

v1 whole, which is shorter than its diff:
```python
import functools
import math

import jax
import jax.numpy as jnp
from jax import lax
from jax.experimental import pallas as pl
from jax.experimental.pallas import tpu as pltpu
from jax.sharding import Mesh
from jax.sharding import PartitionSpec as P

DK = 128
DV = 256
BT = 256
NW = 3 * DK + DV
SEQ = ("seq_0", "seq_1", "seq_2")
SEQ_TP = ("seq_0", "seq_1", "seq_2", "tp")
MESH = pl.DeviceIdType.MESH
F32 = jnp.float32
BF16 = jnp.bfloat16


def mm(a, b):
    return lax.dot_general(a, b, (((1,), (0,)), ((), ())), preferred_element_type=F32)


def mm_nt(a, b):
    return lax.dot_general(a, b, (((1,), (1,)), ((), ())), preferred_element_type=F32)


def mm_tn(a, b):
    return lax.dot_general(a, b, (((0,), (0,)), ((), ())), preferred_element_type=F32)


def split(a):
    high = a.astype(BF16)
    return high, (a - high.astype(F32)).astype(BF16)


def body(dims, signal_scale, tok_hbm, wq, wk, wv, wg, rate_ref, og_hbm, gs_hbm, all_hbm,
         w_s, tok_s, og_s, qt, kt, vs, cs, sq, tri, carry, spre, gpre, dmsg, dpart, zsend, zrecv, zexc,
         xsend, xrecv, fsend, frecv, psend, states, gbuf, rbuf, gsb, allb,
         load_sem, tok_sem, d_sem, z_sem, x_sem, f_sem, p_sem, a_sem, out_sem):
    nx, nz, ny, rows, width, blocks = dims
    x, z, c, y = (lax.axis_index(a) for a in SEQ_TP)
    sgn = 1 - 2 * c
    per_chunk = blocks // ny
    quarter = DV // nz
    pairs = blocks // 2

    barrier = pltpu.get_barrier_semaphore()
    xrecv[...] = jnp.zeros_like(xrecv)
    peers = [{"seq_2": 1 - c}]
    peers += [{"seq_0": lax.rem(x + d, nx)} for d in range(1, nx)]
    peers += [{"seq_1": lax.rem(z + d, nz)} for d in range(1, nz)]
    peers += [{"tp": lax.rem(y + d, ny)} for d in range(1, ny)]
    for peer in peers:
        pl.semaphore_signal(barrier, inc=1, device_id=peer, device_id_type=MESH)

    loads = [
        pltpu.make_async_copy(wq, w_s.at[:, pl.ds(0, DK)], load_sem.at[0]),
        pltpu.make_async_copy(wk, w_s.at[:, pl.ds(DK, DK)], load_sem.at[1]),
        pltpu.make_async_copy(wv, w_s.at[:, pl.ds(2 * DK, DV)], load_sem.at[2]),
        pltpu.make_async_copy(wg, w_s.at[:, pl.ds(2 * DK + DV, DK)], load_sem.at[3]),
        pltpu.make_async_copy(og_hbm, og_s, load_sem.at[4]),
    ]

    def tok_copy(i):
        slot = lax.rem(i, 2)
        start = pl.multiple_of(i * 2 * BT, 2 * BT)
        return pltpu.make_async_copy(tok_hbm.at[pl.ds(start, 2 * BT)], tok_s.at[slot], tok_sem.at[slot])

    tok_copy(0).start()
    for load in loads:
        load.start()

    at = lax.broadcasted_iota(jnp.int32, (BT, BT), 0)
    before = lax.broadcasted_iota(jnp.int32, (BT, BT), 1)
    tri[0] = (at >= before).astype(F32).astype(BF16)
    tri[1] = (at <= before).astype(F32).astype(BF16)
    carry[...] = jnp.zeros_like(carry)
    spre[0] = jnp.zeros((DV, DK), F32)
    gpre[0] = jnp.zeros((DV, DK), F32)
    rate = rate_ref[...]
    for load in loads:
        load.wait()

    @pl.loop(0, pairs)
    def _(i):
        slot = lax.rem(i, 2)

        @pl.when(i + 1 < pairs)
        def _():
            tok_copy(i + 1).start()

        tok_copy(i).wait()
        here = tok_s[slot]
        qk = mm(here, w_s[:, 0:2 * DK])
        val = mm(here, w_s[:, 2 * DK:2 * DK + DV])
        gate = mm(here, w_s[:, 2 * DK + DV:])
        for half in range(2):
            b = i * 2 + half
            at_rows = pl.ds(pl.multiple_of(b * BT, BT), BT)
            part = slice(half * BT, (half + 1) * BT)
            squashed = jax.nn.sigmoid(gate[part])
            sq[at_rows, :] = squashed
            high, low = split(-rate * squashed)
            running = mm(tri[0], high) + mm(tri[0], low) + carry[0:1, :]
            carry[0:1, :] = running[BT - 1:BT, :]
            cs[at_rows, :] = running
            q_here = qk[part, 0:DK].astype(BF16).astype(F32)
            k_here = qk[part, DK:2 * DK].astype(BF16).astype(F32)
            q_run = (q_here * jnp.exp(running)).astype(BF16)
            k_run = (k_here * jnp.exp(-running)).astype(BF16)
            v_here = val[part].astype(BF16)
            qt[at_rows, :] = q_run
            kt[at_rows, :] = k_run
            vs[at_rows, :] = v_here
            spre[b + 1] = spre[b] + mm_tn(v_here, k_run)
            gpre[b + 1] = gpre[b] + mm_tn(og_s[at_rows, :], q_run)

    log_total = carry[0:1, :]
    decay = jnp.exp(log_total)
    dmsg[0, 0:DV, :] = spre[blocks] * decay
    dmsg[1, 0:DV, :] = gpre[blocks]
    for kind in range(2):
        dmsg[kind, DV:DV + 8, :] = jnp.broadcast_to(log_total, (8, DK))
    pl.semaphore_wait(barrier, len(peers))

    d_copy = pltpu.make_async_remote_copy(
        dmsg.at[1 - c], dpart, d_sem.at[0], d_sem.at[1], device_id={"seq_2": 1 - c}, device_id_type=MESH)
    d_copy.start()
    d_copy.wait()
    chip_log = log_total + dpart[DV:DV + 1, :]
    chip = dpart[0:DV, :] + jnp.exp(dpart[DV:DV + 1, :]) * dmsg[c, 0:DV, :]
    for n in range(nz):
        zsend[n, 0:quarter, :] = chip[n * quarter:(n + 1) * quarter, :]
        zsend[n, quarter:quarter + 8, :] = jnp.broadcast_to(chip_log, (8, DK))
    zrecv[z] = zsend[z]
    z_copies = []
    for d in range(1, nz):
        to = lax.rem(z + d, nz)
        z_copies.append(pltpu.make_async_remote_copy(
            zsend.at[to], zrecv.at[z], z_sem.at[0, d - 1], z_sem.at[1, d - 1],
            device_id={"seq_1": to}, device_id_type=MESH))
    for copy in z_copies:
        copy.start()
    for copy in z_copies:
        copy.wait()
    total = jnp.zeros((quarter, DK), F32)
    total_log = jnp.zeros((1, DK), F32)
    for n in range(nz):
        src = c * (nz - 1) + sgn * n
        zexc[src, 0:quarter, :] = total
        zexc[src, quarter:quarter + 8, :] = jnp.broadcast_to(total_log, (8, DK))
        log_here = zrecv[src, quarter:quarter + 1, :]
        total = zrecv[src, 0:quarter, :] + jnp.exp(log_here) * total
        total_log = total_log + log_here
    xsend[0:quarter, :] = total
    xsend[quarter:quarter + 8, :] = jnp.broadcast_to(total_log, (8, DK))

    def x_copy(d):
        to = x + sgn * d
        inside = (to >= 0) & (to < nx)
        return inside, pltpu.make_async_remote_copy(
            xsend, xrecv.at[d - 1], x_sem.at[0, d - 1], x_sem.at[1, d - 1],
            device_id={"seq_0": jnp.where(inside, to, 1 - jnp.minimum(x, 1))}, device_id_type=MESH)

    for d in range(1, nx):
        inside, copy = x_copy(d)
        pl.when(inside)(copy.start)
    for d in range(1, nx):
        inside, copy = x_copy(d)
        pl.when(inside)(copy.wait_send)
        source = x - sgn * d
        pl.when((source >= 0) & (source < nx))(copy.wait_recv)
    entering = jnp.zeros((quarter, DK), F32)
    for d in reversed(range(1, nx)):
        entering = xrecv[d - 1, 0:quarter, :] + jnp.exp(xrecv[d - 1, quarter:quarter + 1, :]) * entering
    for n in range(nz):
        fsend[n] = zexc[n, 0:quarter, :] + jnp.exp(zexc[n, quarter:quarter + 1, :]) * entering
    frecv[z] = fsend[z]
    f_copies = []
    for d in range(1, nz):
        to = lax.rem(z + d, nz)
        f_copies.append(pltpu.make_async_remote_copy(
            fsend.at[to], frecv.at[z], f_sem.at[0, d - 1], f_sem.at[1, d - 1],
            device_id={"seq_1": to}, device_id_type=MESH))
    for copy in f_copies:
        copy.start()
    for copy in f_copies:
        copy.wait()
    entered = frecv[...].reshape(DV, DK)
    psend[...] = dmsg[c, 0:DV, :] + decay * entered
    states[c] = entered
    p_copy = pltpu.make_async_remote_copy(
        psend, states.at[c], p_sem.at[0], p_sem.at[1], device_id={"seq_2": 1 - c}, device_id_type=MESH)
    p_copy.start()
    p_copy.wait()
    states[1] = states[1] * decay

    def a_copy(n):
        o = lax.rem(n // per_chunk + 1, ny)
        i = lax.rem(n, per_chunk)
        to = lax.rem(y + o, ny)
        b = to * per_chunk + i
        return o, i, to, b

    def start_send(n):
        o, i, to, b = a_copy(n)
        dst = pl.ds(pl.multiple_of(i * BT, BT), BT)
        slot = o - 1
        return pltpu.make_async_remote_copy(
            gbuf.at[b], rbuf.at[slot, dst], a_sem.at[0, slot, i], a_sem.at[1, slot, i],
            device_id={"tp": to}, device_id_type=MESH)

    remote = blocks - per_chunk

    @pl.loop(0, blocks)
    def _(n):
        o, i, to, b = a_copy(n)
        at_rows = pl.ds(pl.multiple_of(b * BT, BT), BT)
        q_run = qt[at_rows, :]
        k_run = kt[at_rows, :]
        v_here = vs[at_rows, :]
        o_grad = og_s[at_rows, :]
        running = cs[at_rows, :]
        squashed = sq[at_rows, :]
        upper = tri[1].astype(F32)
        lower = tri[0].astype(F32)
        scores_t = (mm_nt(k_run, q_run) * upper).astype(BF16)
        d_scores = (mm_nt(o_grad, v_here) * lower).astype(BF16)
        d_scores_t = (mm_nt(v_here, o_grad) * upper).astype(BF16)
        state = states[0] + spre[b]
        after = states[0] + spre[b + 1]
        cotangent = states[1] + (gpre[blocks] - gpre[b + 1])
        state_low = state.astype(BF16)
        cot_low = cotangent.astype(BF16)
        dv = mm(scores_t, o_grad) + mm_nt(k_run, cot_low)
        dq = mm(o_grad, state_low) + mm(d_scores, k_run)
        dk = mm(v_here, cot_low) + mm(d_scores_t, q_run)
        boundary = jnp.sum(after * cotangent, axis=0, keepdims=True)
        high, low = split(q_run.astype(F32) * dq - k_run.astype(F32) * dk)
        dg = mm(tri[1], high) + mm(tri[1], low) + boundary
        pre = dg * (-rate) * squashed * (1.0 - squashed)
        gsb[at_rows, :] = pre * signal_scale
        gbuf[b, :, 0:DK] = dq * jnp.exp(running)
        gbuf[b, :, DK:2 * DK] = dk * jnp.exp(-running)
        gbuf[b, :, 2 * DK:2 * DK + DV] = dv
        gbuf[b, :, 2 * DK + DV:] = pre

        @pl.when((n >= 1) & (n - 1 < remote))
        def _():
            start_send(n - 1).start()

    gs_copy = pltpu.make_async_copy(gsb, gs_hbm, out_sem.at[0])
    gs_copy.start()
    for i in range(per_chunk):
        allb[i * BT:(i + 1) * BT, pl.ds(pl.multiple_of(y * NW, 128), NW)] = gbuf[y * per_chunk + i].astype(BF16)

    @pl.loop(0, remote)
    def _(n):
        copy = start_send(n)
        copy.wait_send()
        copy.wait_recv()

    for o in range(1, ny):
        head = lax.rem(y - o + ny, ny)
        allb[:, pl.ds(pl.multiple_of(head * NW, 128), NW)] = rbuf[o - 1].astype(BF16)
    all_copy = pltpu.make_async_copy(allb, all_hbm, out_sem.at[1])
    all_copy.start()
    all_copy.wait()
    gs_copy.wait()


def mix_body(g_ref, w_ref, o_ref):
    heads = w_ref.shape[0]
    total = None
    for h in range(heads):
        term = mm_nt(g_ref[:, h * NW:(h + 1) * NW], w_ref[h].astype(BF16))
        total = term if total is None else total + term
    o_ref[...] = total.astype(BF16)


def per_device(dims, tokens, w_query, w_key, w_value, w_gate, gate_rate, out_grad):
    nx, nz, ny = dims
    rows, width = tokens.shape
    blocks = rows // BT
    mine = rows // ny
    quarter = DV // nz
    whole_tokens = rows * nx * nz * 2
    signal_scale = 4.0 * math.sqrt(whole_tokens * DK / DV)

    spot = (lax.axis_index("seq_0") * nz + lax.axis_index("seq_1")) * 2 + lax.axis_index("seq_2")
    share = width // (nx * nz * 2)
    pieces = [lax.dynamic_slice_in_dim(w, spot * share, share, 0) for w in (w_query, w_key, w_value, w_gate)]
    piece = jnp.concatenate(pieces, axis=1).astype(F32)
    gathered = lax.all_gather(piece, "tp")
    gathered = lax.all_gather(gathered, SEQ, axis=1, tiled=True)

    any_spec = pl.BlockSpec(memory_space=pl.ANY)
    vmem_spec = pl.BlockSpec(memory_space=pltpu.VMEM)
    dma = pltpu.SemaphoreType.DMA
    signal, grads = pl.pallas_call(
        functools.partial(body, (nx, nz, ny, rows, width, blocks), signal_scale),
        out_shape=(
            jax.ShapeDtypeStruct((rows, DK), F32),
            jax.ShapeDtypeStruct((mine, ny * NW), BF16),
        ),
        in_specs=[any_spec] * 5 + [vmem_spec, any_spec],
        out_specs=(any_spec, any_spec),
        scratch_shapes=[
            pltpu.VMEM((width, NW), BF16),
            pltpu.VMEM((2, 2 * BT, width), BF16),
            pltpu.VMEM((rows, DV), BF16),
            pltpu.VMEM((rows, DK), BF16),
            pltpu.VMEM((rows, DK), BF16),
            pltpu.VMEM((rows, DV), BF16),
            pltpu.VMEM((rows, DK), F32),
            pltpu.VMEM((rows, DK), F32),
            pltpu.VMEM((2, BT, BT), BF16),
            pltpu.VMEM((8, DK), F32),
            pltpu.VMEM((blocks + 1, DV, DK), F32),
            pltpu.VMEM((blocks + 1, DV, DK), F32),
            pltpu.VMEM((2, DV + 8, DK), F32),
            pltpu.VMEM((DV + 8, DK), F32),
            pltpu.VMEM((nz, quarter + 8, DK), F32),
            pltpu.VMEM((nz, quarter + 8, DK), F32),
            pltpu.VMEM((nz, quarter + 8, DK), F32),
            pltpu.VMEM((quarter + 8, DK), F32),
            pltpu.VMEM((nx - 1, quarter + 8, DK), F32),
            pltpu.VMEM((nz, quarter, DK), F32),
            pltpu.VMEM((nz, quarter, DK), F32),
            pltpu.VMEM((DV, DK), F32),
            pltpu.VMEM((2, DV, DK), F32),
            pltpu.VMEM((blocks, BT, NW), F32),
            pltpu.VMEM((ny - 1, mine, NW), F32),
            pltpu.VMEM((rows, DK), F32),
            pltpu.VMEM((mine, ny * NW), BF16),
            dma((5,)),
            dma((2,)),
            dma((2,)),
            dma((2, nz - 1)),
            dma((2, nx - 1)),
            dma((2, nz - 1)),
            dma((2,)),
            dma((2, ny - 1, blocks // ny)),
            dma((2,)),
        ],
        compiler_params=pltpu.CompilerParams(
            collective_id=0, has_side_effects=True, vmem_limit_bytes=60 * 2**20),
        cost_estimate=pl.CostEstimate(
            flops=40_000_000_000, bytes_accessed=30_000_000, transcendentals=1_000_000),
    )(tokens, w_query, w_key, w_value, w_gate, gate_rate.reshape(1, DK), out_grad)

    tile = 128
    mixed = pl.pallas_call(
        mix_body,
        grid=(width // tile,),
        out_shape=jax.ShapeDtypeStruct((mine, width), BF16),
        in_specs=[
            pl.BlockSpec((mine, ny * NW), lambda i: (0, 0)),
            pl.BlockSpec((ny, tile, NW), lambda i: (0, i, 0)),
        ],
        out_specs=pl.BlockSpec((mine, tile), lambda i: (0, i)),
    )(grads, gathered)
    return mixed, signal


def solution(mesh, shape=(4, 4)):
    nx, nz = shape
    ny = mesh.shape["tp"]
    torus = Mesh(mesh.devices.reshape(nx, nz, 2, ny), SEQ_TP)
    placed = (
        P(SEQ, None),
        P(None, "tp"),
        P(None, "tp"),
        P(None, "tp"),
        P(None, "tp"),
        P("tp"),
        P(SEQ, "tp"),
    )
    return jax.shard_map(
        functools.partial(per_device, (nx, nz, ny)),
        mesh=torus,
        in_specs=placed,
        out_specs=(P(SEQ_TP, None), P(SEQ, "tp")),
        check_vma=False,
    )
```

time: 739 us -> 159 us (0.22); the launches traced: 727 us -> 159 us
  matrix products: 256 us -> 0 us
  waiting for transfers between devices: 191 us -> 1.71 us
  other arithmetic: 131 us -> 0.02 us
  Pallas kernels: 0 us -> 126 us
  blocking collectives: 75.9 us -> 13.7 us
  local copies, waits for them, and re-layouts: 56.9 us -> 3.24 us
    dot_general x170 -> x0, matrix products: 256 us -> none  [the longest x160 177 us: low_dot(): jnp.dot(left.astype(jnp.bfloat16), right.astype(jnp.bfloat16), preferred_...]
    reduce_scatter x1 -> x0, waiting for transfers between devices: 191 us -> none  [per_device(): lax.psum_scatter(term(tokens.shape[0] // lax.axis_size('tp') * lax.axis_s...]
    pallas_call x0 -> x2, Pallas kernels: none -> 126 us  [the longest x1 100 us: per_device(): pl.pallas_call(functools.partial(body, (nx, nz, ny, rows, width, blocks),...]
    dynamic_update_slice x64 -> x0, other arithmetic: 82.4 us -> none  [run_head(): last_memory, outputs = lax.scan(advance, initial, pieces)]
    all_gather x10 -> x1, blocking collectives: 75.9 us -> 13.7 us  [per_device(): gathered = lax.all_gather(piece, 'tp')]
    another operation x58 -> x0, other arithmetic: 37.5 us -> none  [the longest x48 36.8 us: advance(): within = jnp.cumsum(gate_block, axis=0)]
    dynamic_update_slice x64 -> x0, local copies, waits for them, and re-layouts: 21.2 us -> none  [run_head(): last_memory, outputs = lax.scan(advance, initial, pieces)]
    dynamic_slice x32 -> x0, local copies, waits for them, and re-layouts: 16.1 us -> none  [run_head(): last_memory, outputs = lax.scan(advance, initial, pieces)]
  transfers between devices with their start and end apart: 1 -> 1, of which waited for: 1 -> 1; matrix products, arithmetic and copies ran while one was open for 0% -> 0% of each run, Pallas kernels for 0% -> 63%
where the time goes in v1:
time: 159 us
  Pallas kernels  126 us (79%)
  between operations  14 us (9%)
  blocking collectives  13.7 us (9%)
  local copies, waits for them, and re-layouts  3.24 us (2%)
  waiting for transfers between devices  1.71 us (1%)
    pallas_call x1, Pallas kernels, per_device(): pl.pallas_call(functools.partial(body, (nx, nz, ny, rows, width, blocks),...  100 us
    pallas_call x1, Pallas kernels, per_device(): pl.pallas_call(mix_body, grid=(width // tile,), out_shape=jax.ShapeDtypeS...  25.4 us
    all_gather x1, blocking collectives, per_device(): gathered = lax.all_gather(piece, 'tp')  13.7 us
  transfers between devices with their start and end apart: 1, of which 1 were waited for; matrix products, arithmetic and copies ran while one was open for 0% of the time, Pallas kernels for 63%

profile of v1, /device:TPU:1, one launch (start us, length us, event | category | flops | bytes accessed | tf_op | source)
XLA Modules:
  0.0 158.6 jit_solution(14945555887486632298)
XLA Ops:
  7.2 0.0 all-gather.2.cloned.1.call-start
  7.2 0.7 dynamic-slice_bitcast_fusion.3
  8.0 0.8 dynamic-slice_bitcast_fusion
  8.7 0.7 dynamic-slice_bitcast_fusion.1
  9.5 13.7 %all_gather.7 = f32[4,80,640]{2,1,0:T(8,128)} all-gather(f32[1,80,640]{2,1,0:T(8,128)S(1)} %maximum_convert_fusion), channel_id=1, replica_groups=mesh['seq_0'=4,'seq_1'=4,'seq_2'=2,'tp'=4] {'tp'}, dimensions={0}, use_global_device_ids=true | all-gather | bytes 1024000 | tf_op jit(solution)/shard_map/all_gather | solution.py:298
  23.2 0.0 all-gather.2.cloned.1.call-update
  23.2 100.5 %shard_map.86 = (f32[2048,128]{1,0:T(8,128)}, bf16[512,2560]{1,0:T(8,128)(2,1)}) custom-call(bf16[2048,2560]{1,0:T(8,128)(2,1)} %tok_hbm.1, bf16[2560,128]{1,0:T(8,128)(2,1)} %wq.1, bf16[2560,128]{1,0:T(8,128)(2,1)} %wk.1, bf16[2560,256]{1,0:T(8,128)(2,1)} %wv.1, bf16[2560,128]{1,0:T(8,128)(2,1)} %wg.1, f32[1,128]{1,0:T(1,128)} %bitcast.9, ...), custom_call_target="tpu_custom_call" | custom-call | flops 40000000000 | bytes 30000000 | tf_op jit(solution)/shard_map/pallas_call | solution.py:304
  123.7 1.7 %all-gather.2.cloned.1.call-done.w_ref = f32[4,2560,640]{2,1,0:T(8,128)} async-done(((f32[4,80,640]{2,1,0:T(8,128)}), f32[4,2560,640]{2,1,0:T(8,128)}) %all-gather.2.cloned.1.call-update) | async-done | bytes 26214416 | tf_op jit(solution)/shard_map/all_gather | solution.py:299
  125.4 0.0 copy-start
  125.4 25.4 %shard_map.87 = bf16[512,2560]{1,0:T(8,128)(2,1)} custom-call(bf16[512,2560]{1,0:T(8,128)(2,1)} %get-tuple-element.4.g_ref, f32[4,2560,640]{2,1,0:T(8,128)} %all-gather.2.cloned.1.call-done.w_ref), custom_call_target="tpu_custom_call" | custom-call | tf_op jit(solution)/shard_map/pallas_call | solution.py:357
  150.8 0.0 copy-done
  150.8 1.0 copy.10
  (1 shorter events, 0.0 us)
Async XLA Ops:
  7.2 118.2 %all-gather.2.cloned.1.call-start = ((), (), s32[]{:S(2)}) async-start(), calls=%async_computation | async-start | bytes 27033600 | tf_op jit(solution)/shard_map/all_gather | solution.py:299
  125.4 25.4 %copy-start = (f32[2048,128]{1,0:T(8,128)S(1)}, f32[2048,128]{1,0:T(8,128)}, u32[]{:S(2)}) copy-start(f32[2048,128]{1,0:T(8,128)} %get-tuple-element.11) | copy-start | bytes 3145732
Sparse Core Ops, SparseCore 0:
  23.3 102.0 all-gather.1

commit v2 on v1

v2 whole, which is shorter than its diff:
```python
import functools
import math

import jax
import jax.numpy as jnp
from jax import lax
from jax.experimental import pallas as pl
from jax.experimental.pallas import tpu as pltpu
from jax.sharding import Mesh
from jax.sharding import PartitionSpec as P

DK = 128
DV = 256
BT = 256
NW = 3 * DK + DV
SEQ = ("seq_0", "seq_1", "seq_2")
SEQ_TP = ("seq_0", "seq_1", "seq_2", "tp")
MESH = pl.DeviceIdType.MESH
F32 = jnp.float32
BF16 = jnp.bfloat16


def mm(a, b):
    return lax.dot_general(a, b, (((1,), (0,)), ((), ())), preferred_element_type=F32)


def mm_nt(a, b):
    return lax.dot_general(a, b, (((1,), (1,)), ((), ())), preferred_element_type=F32)


def mm_tn(a, b):
    return lax.dot_general(a, b, (((0,), (0,)), ((), ())), preferred_element_type=F32)


def split(a):
    high = a.astype(BF16)
    return high, (a - high.astype(F32)).astype(BF16)


def body(dims, signal_scale, tok_hbm, wq, wk, wv, wg, rate_ref, og_hbm, out_hbm, gs_hbm,
         w_s, tok_s, og_s, qt, kt, vs, cs, sq, tri, carry, spre, gpre, dmsg, dpart, zsend, zrecv, zexc,
         xsend, xrecv, fsend, frecv, psend, states, gbuf, rbuf, gsb, acc, wsend, wl,
         load_sem, tok_sem, d_sem, z_sem, x_sem, f_sem, p_sem, a_sem, out_sem,
         wy_sem, w1_sem, f1_sem, w2_sem, f2_sem, wd_sem):
    nx, nz, ny, rows, width, blocks = dims
    x, z, c, y = (lax.axis_index(a) for a in SEQ_TP)
    sgn = 1 - 2 * c
    per_chunk = blocks // ny
    quarter = DV // nz
    pairs = blocks // 2
    mine = rows // ny

    ring = nx
    share = width // (ring * ring * 2)
    first = x + c * (z - x)
    second = z + c * (x - z)

    def place(a, b):
        return {"seq_0": a + c * (b - a), "seq_1": b + c * (a - b)}

    def wrap(v):
        return lax.rem(v + ring, ring)

    def share_at(a, b, part, parts):
        size = share // parts
        start = ((c * ring + a) * ring + b) * share + part * size
        return pl.ds(pl.multiple_of(start, 8), size)

    def group_at(a, part, parts):
        size = ring * share // parts
        start = (c * ring + a) * ring * share + part * size
        return pl.ds(pl.multiple_of(start, 8), size)

    def remote(src, dst, sems, i, to):
        return pltpu.make_async_remote_copy(
            src, dst, sems.at[(0, *i)], sems.at[(1, *i)], device_id=to, device_id_type=MESH)

    def wy_copy(o):
        dst = wl.at[o - 1, share_at(first, second, 0, 1)]
        return remote(wsend, dst, wy_sem, (o - 1,), {"tp": lax.rem(y + o, ny)})

    turns = (0, 1) if ring > 2 else (0,)

    def w1_copy(s, turn):
        ref = wl.at[s, share_at(first, second, 0, 1)]
        return remote(ref, ref, w1_sem, (s, turn), place(first, wrap(second + 1 - 2 * turn)))

    def f1_copy(s, turn):
        ref = wl.at[s, share_at(first, wrap(second - 1 + 2 * turn), turn, 2)]
        return remote(ref, ref, f1_sem, (s, turn), place(first, wrap(second + 1 - 2 * turn)))

    def w2_copy(s, turn):
        ref = wl.at[s, group_at(first, 0, 1)]
        return remote(ref, ref, w2_sem, (s, turn), place(wrap(first + 1 - 2 * turn), second))

    def f2_copy(s, turn):
        ref = wl.at[s, group_at(wrap(first - 1 + 2 * turn), turn, 2)]
        return remote(ref, ref, f2_sem, (s, turn), place(wrap(first + 1 - 2 * turn), second))

    def wd_copy(s, n):
        ref = wl.at[s, group_at(lax.rem(first + n, ring), 0, 1)]
        return remote(ref, ref, wd_sem, (s, n), {"seq_2": 1 - c})

    def start_all(copy, s):
        for turn in turns:
            copy(s, turn).start()

    def arrive_all(copy, s):
        for turn in turns:
            copy(s, turn).wait_recv()

    barrier = pltpu.get_barrier_semaphore()
    xrecv[...] = jnp.zeros_like(xrecv)
    peers = [{"seq_2": 1 - c}]
    peers += [{"seq_0": lax.rem(x + d, nx)} for d in range(1, nx)]
    peers += [{"seq_1": lax.rem(z + d, nz)} for d in range(1, nz)]
    peers += [{"tp": lax.rem(y + d, ny)} for d in range(1, ny)]
    for peer in peers:
        pl.semaphore_signal(barrier, inc=1, device_id=peer, device_id_type=MESH)

    loads = [
        pltpu.make_async_copy(wq, w_s.at[:, pl.ds(0, DK)], load_sem.at[0]),
        pltpu.make_async_copy(wk, w_s.at[:, pl.ds(DK, DK)], load_sem.at[1]),
        pltpu.make_async_copy(wv, w_s.at[:, pl.ds(2 * DK, DV)], load_sem.at[2]),
        pltpu.make_async_copy(wg, w_s.at[:, pl.ds(2 * DK + DV, DK)], load_sem.at[3]),
        pltpu.make_async_copy(og_hbm, og_s, load_sem.at[4]),
    ]

    def tok_copy(i):
        slot = lax.rem(i, 2)
        start = pl.multiple_of(i * 2 * BT, 2 * BT)
        return pltpu.make_async_copy(tok_hbm.at[pl.ds(start, 2 * BT)], tok_s.at[slot], tok_sem.at[slot])

    tok_copy(0).start()
    for load in loads:
        load.start()

    at = lax.broadcasted_iota(jnp.int32, (BT, BT), 0)
    before = lax.broadcasted_iota(jnp.int32, (BT, BT), 1)
    tri[0] = (at >= before).astype(F32).astype(BF16)
    tri[1] = (at <= before).astype(F32).astype(BF16)
    carry[...] = jnp.zeros_like(carry)
    spre[0] = jnp.zeros((DV, DK), F32)
    gpre[0] = jnp.zeros((DV, DK), F32)
    rate = rate_ref[...]
    for load in loads:
        load.wait()
    wsend[...] = w_s[share_at(first, second, 0, 1), :].astype(F32)
    pl.semaphore_wait(barrier, len(peers))
    for o in range(1, ny):
        wy_copy(o).start()

    with jax.named_scope("proj"):
        @pl.loop(0, pairs)
        def _(i):
            slot = lax.rem(i, 2)

            @pl.when(i + 1 < pairs)
            def _():
                tok_copy(i + 1).start()

            tok_copy(i).wait()
            here = tok_s[slot]
            qk = mm(here, w_s[:, 0:2 * DK])
            val = mm(here, w_s[:, 2 * DK:2 * DK + DV])
            gate = mm(here, w_s[:, 2 * DK + DV:])
            for half in range(2):
                b = i * 2 + half
                at_rows = pl.ds(pl.multiple_of(b * BT, BT), BT)
                part = slice(half * BT, (half + 1) * BT)
                squashed = jax.nn.sigmoid(gate[part])
                sq[at_rows, :] = squashed
                high, low = split(-rate * squashed)
                running = mm(tri[0], high) + mm(tri[0], low) + carry[0:1, :]
                carry[0:1, :] = running[BT - 1:BT, :]
                cs[at_rows, :] = running
                q_here = qk[part, 0:DK].astype(BF16).astype(F32)
                k_here = qk[part, DK:2 * DK].astype(BF16).astype(F32)
                q_run = (q_here * jnp.exp(running)).astype(BF16)
                k_run = (k_here * jnp.exp(-running)).astype(BF16)
                v_here = val[part].astype(BF16)
                qt[at_rows, :] = q_run
                kt[at_rows, :] = k_run
                vs[at_rows, :] = v_here
                spre[b + 1] = spre[b] + mm_tn(v_here, k_run)
                gpre[b + 1] = gpre[b] + mm_tn(og_s[at_rows, :], q_run)


    log_total = carry[0:1, :]
    decay = jnp.exp(log_total)
    dmsg[0, 0:DV, :] = spre[blocks] * decay
    dmsg[1, 0:DV, :] = gpre[blocks]
    for kind in range(2):
        dmsg[kind, DV:DV + 8, :] = jnp.broadcast_to(log_total, (8, DK))

    d_copy = pltpu.make_async_remote_copy(
        dmsg.at[1 - c], dpart, d_sem.at[0], d_sem.at[1], device_id={"seq_2": 1 - c}, device_id_type=MESH)
    with jax.named_scope("d2d"):
        d_copy.start()
        d_copy.wait()

    chip_log = log_total + dpart[DV:DV + 1, :]
    chip = dpart[0:DV, :] + jnp.exp(dpart[DV:DV + 1, :]) * dmsg[c, 0:DV, :]
    for n in range(nz):
        zsend[n, 0:quarter, :] = chip[n * quarter:(n + 1) * quarter, :]
        zsend[n, quarter:quarter + 8, :] = jnp.broadcast_to(chip_log, (8, DK))
    zrecv[z] = zsend[z]
    z_copies = []
    for d in range(1, nz):
        to = lax.rem(z + d, nz)
        z_copies.append(pltpu.make_async_remote_copy(
            zsend.at[to], zrecv.at[z], z_sem.at[0, d - 1], z_sem.at[1, d - 1],
            device_id={"seq_1": to}, device_id_type=MESH))
    for copy in z_copies:
        copy.start()
    slots = [0, 2, 1][: ny - 1] if ny > 2 else [0]
    for s in range(ny - 1):
        wy_copy(s + 1).wait_recv()
    start_all(w1_copy, slots[0])
    with jax.named_scope("zex"):
        for copy in z_copies:
            copy.wait()

    total = jnp.zeros((quarter, DK), F32)
    total_log = jnp.zeros((1, DK), F32)
    for n in range(nz):
        src = c * (nz - 1) + sgn * n
        zexc[src, 0:quarter, :] = total
        zexc[src, quarter:quarter + 8, :] = jnp.broadcast_to(total_log, (8, DK))
        log_here = zrecv[src, quarter:quarter + 1, :]
        total = zrecv[src, 0:quarter, :] + jnp.exp(log_here) * total
        total_log = total_log + log_here
    xsend[0:quarter, :] = total
    xsend[quarter:quarter + 8, :] = jnp.broadcast_to(total_log, (8, DK))

    def x_copy(d):
        to = x + sgn * d
        inside = (to >= 0) & (to < nx)
        return inside, pltpu.make_async_remote_copy(
            xsend, xrecv.at[d - 1], x_sem.at[0, d - 1], x_sem.at[1, d - 1],
            device_id={"seq_0": jnp.where(inside, to, 1 - jnp.minimum(x, 1))}, device_id_type=MESH)

    for d in range(1, nx):
        inside, copy = x_copy(d)
        pl.when(inside)(copy.start)
    for s in slots[1:2]:
        start_all(w1_copy, s)
    with jax.named_scope("xex"):
        for d in range(1, nx):
            inside, copy = x_copy(d)
            pl.when(inside)(copy.wait_send)
            source = x - sgn * d
            pl.when((source >= 0) & (source < nx))(copy.wait_recv)

    entering = jnp.zeros((quarter, DK), F32)
    for d in reversed(range(1, nx)):
        entering = xrecv[d - 1, 0:quarter, :] + jnp.exp(xrecv[d - 1, quarter:quarter + 1, :]) * entering
    for n in range(nz):
        fsend[n] = zexc[n, 0:quarter, :] + jnp.exp(zexc[n, quarter:quarter + 1, :]) * entering
    frecv[z] = fsend[z]
    f_copies = []
    for d in range(1, nz):
        to = lax.rem(z + d, nz)
        f_copies.append(pltpu.make_async_remote_copy(
            fsend.at[to], frecv.at[z], f_sem.at[0, d - 1], f_sem.at[1, d - 1],
            device_id={"seq_1": to}, device_id_type=MESH))
    for copy in f_copies:
        copy.start()
    for s in slots[2:]:
        start_all(w1_copy, s)
    with jax.named_scope("fex"):
        for copy in f_copies:
            copy.wait()

    entered = frecv[...].reshape(DV, DK)
    psend[...] = dmsg[c, 0:DV, :] + decay * entered
    states[c] = entered
    p_copy = pltpu.make_async_remote_copy(
        psend, states.at[c], p_sem.at[0], p_sem.at[1], device_id={"seq_2": 1 - c}, device_id_type=MESH)
    with jax.named_scope("pex"):
        p_copy.start()
        p_copy.wait()

    states[1] = states[1] * decay
    for s in slots:
        arrive_all(w1_copy, s)
        if ring > 2:
            start_all(f1_copy, s)

    def a_copy(n):
        o = lax.rem(n // per_chunk + 1, ny)
        i = lax.rem(n, per_chunk)
        to = lax.rem(y + o, ny)
        b = to * per_chunk + i
        return o, i, to, b

    def start_send(n):
        o, i, to, b = a_copy(n)
        dst = pl.ds(pl.multiple_of(i * BT, BT), BT)
        slot = o - 1
        return pltpu.make_async_remote_copy(
            gbuf.at[b], rbuf.at[slot, dst], a_sem.at[0, slot, i], a_sem.at[1, slot, i],
            device_id={"tp": to}, device_id_type=MESH)

    sent = blocks - per_chunk

    with jax.named_scope("blk"):
        @pl.loop(0, blocks)
        def _(n):
            o, i, to, b = a_copy(n)
            at_rows = pl.ds(pl.multiple_of(b * BT, BT), BT)
            q_run = qt[at_rows, :]
            k_run = kt[at_rows, :]
            v_here = vs[at_rows, :]
            o_grad = og_s[at_rows, :]
            running = cs[at_rows, :]
            squashed = sq[at_rows, :]
            upper = tri[1].astype(F32)
            lower = tri[0].astype(F32)
            scores_t = (mm_nt(k_run, q_run) * upper).astype(BF16)
            d_scores = (mm_nt(o_grad, v_here) * lower).astype(BF16)
            d_scores_t = (mm_nt(v_here, o_grad) * upper).astype(BF16)
            state = states[0] + spre[b]
            after = states[0] + spre[b + 1]
            cotangent = states[1] + (gpre[blocks] - gpre[b + 1])
            state_low = state.astype(BF16)
            cot_low = cotangent.astype(BF16)
            dv = mm(scores_t, o_grad) + mm_nt(k_run, cot_low)
            dq = mm(o_grad, state_low) + mm(d_scores, k_run)
            dk = mm(v_here, cot_low) + mm(d_scores_t, q_run)
            boundary = jnp.sum(after * cotangent, axis=0, keepdims=True)
            high, low = split(q_run.astype(F32) * dq - k_run.astype(F32) * dk)
            dg = mm(tri[1], high) + mm(tri[1], low) + boundary
            pre = dg * (-rate) * squashed * (1.0 - squashed)
            gsb[at_rows, :] = pre * signal_scale
            gbuf[b, :, 0:DK] = dq * jnp.exp(running)
            gbuf[b, :, DK:2 * DK] = dk * jnp.exp(-running)
            gbuf[b, :, 2 * DK:2 * DK + DV] = dv
            gbuf[b, :, 2 * DK + DV:] = pre

            @pl.when((n >= 1) & (n - 1 < sent))
            def _():
                start_send(n - 1).start()

            @pl.when(n == 2)
            def _():
                for s in slots:
                    if ring > 2:
                        arrive_all(f1_copy, s)
                    start_all(w2_copy, s)


    gs_copy = pltpu.make_async_copy(gsb, gs_hbm, out_sem.at[0])
    gs_copy.start()
    cols = min(512, width)

    def mix(grads, weights, last):
        @pl.loop(0, width // cols)
        def _(i):
            at = pl.ds(pl.multiple_of(i * cols, cols), cols)
            term = mm_nt(grads, weights(at))
            if last is None:
                acc[:, at] = term
            elif last:
                tok_s[0, 0:mine, at] = (acc[:, at] + term).astype(BF16)
            else:
                acc[:, at] = acc[:, at] + term

    with jax.named_scope("mix_own"):
        own = gbuf[pl.ds(y * per_chunk, per_chunk)].reshape(mine, NW).astype(BF16)
        mix(own, lambda at: w_s[at, :], None)
    with jax.named_scope("weights"):
        for s in slots:
            for n in range(1):
                wd_copy(s, n).start()
        for s in slots:
            arrive_all(w2_copy, s)
            if ring > 2:
                start_all(f2_copy, s)
            wd_copy(s, 1).start()
            if ring > 2:
                wd_copy(s, ring - 1).start()
        if ring > 2:
            for s in slots:
                arrive_all(f2_copy, s)
                wd_copy(s, 2).start()
        for s in slots:
            for n in range(ring):
                wd_copy(s, n).wait_recv()
    for s in slots:
        with jax.named_scope("grads"):
            for i in range(per_chunk):
                start_send(s * per_chunk + i).wait_recv()
        with jax.named_scope("mix"):
            mix(rbuf[s].astype(BF16), lambda at: wl[s, at, :].astype(BF16), s == slots[-1])
    out_copy = pltpu.make_async_copy(tok_s.at[0, pl.ds(0, mine)], out_hbm, out_sem.at[1])
    out_copy.start()
    for o in range(1, ny):
        wy_copy(o).wait_send()
    for s in slots:
        for turn in turns:
            w1_copy(s, turn).wait_send()
            w2_copy(s, turn).wait_send()
            if ring > 2:
                f1_copy(s, turn).wait_send()
                f2_copy(s, turn).wait_send()
        for n in range(ring):
            wd_copy(s, n).wait_send()

    @pl.loop(0, sent)
    def _(n):
        start_send(n).wait_send()

    out_copy.wait()
    gs_copy.wait()


def per_device(dims, tokens, w_query, w_key, w_value, w_gate, gate_rate, out_grad):
    nx, nz, ny = dims
    rows, width = tokens.shape
    blocks = rows // BT
    mine = rows // ny
    quarter = DV // nz
    whole_tokens = rows * nx * nz * 2
    signal_scale = 4.0 * math.sqrt(whole_tokens * DK / DV)

    any_spec = pl.BlockSpec(memory_space=pl.ANY)
    vmem_spec = pl.BlockSpec(memory_space=pltpu.VMEM)
    dma = pltpu.SemaphoreType.DMA
    mixed, signal = pl.pallas_call(
        functools.partial(body, (nx, nz, ny, rows, width, blocks), signal_scale),
        out_shape=(
            jax.ShapeDtypeStruct((mine, width), BF16),
            jax.ShapeDtypeStruct((rows, DK), F32),
        ),
        in_specs=[any_spec] * 5 + [vmem_spec, any_spec],
        out_specs=(any_spec, any_spec),
        scratch_shapes=[
            pltpu.VMEM((width, NW), BF16),
            pltpu.VMEM((2, 2 * BT, width), BF16),
            pltpu.VMEM((rows, DV), BF16),
            pltpu.VMEM((rows, DK), BF16),
            pltpu.VMEM((rows, DK), BF16),
            pltpu.VMEM((rows, DV), BF16),
            pltpu.VMEM((rows, DK), F32),
            pltpu.VMEM((rows, DK), F32),
            pltpu.VMEM((2, BT, BT), BF16),
            pltpu.VMEM((8, DK), F32),
            pltpu.VMEM((blocks + 1, DV, DK), F32),
            pltpu.VMEM((blocks + 1, DV, DK), F32),
            pltpu.VMEM((2, DV + 8, DK), F32),
            pltpu.VMEM((DV + 8, DK), F32),
            pltpu.VMEM((nz, quarter + 8, DK), F32),
            pltpu.VMEM((nz, quarter + 8, DK), F32),
            pltpu.VMEM((nz, quarter + 8, DK), F32),
            pltpu.VMEM((quarter + 8, DK), F32),
            pltpu.VMEM((nx - 1, quarter + 8, DK), F32),
            pltpu.VMEM((nz, quarter, DK), F32),
            pltpu.VMEM((nz, quarter, DK), F32),
            pltpu.VMEM((DV, DK), F32),
            pltpu.VMEM((2, DV, DK), F32),
            pltpu.VMEM((blocks, BT, NW), F32),
            pltpu.VMEM((ny - 1, mine, NW), F32),
            pltpu.VMEM((rows, DK), F32),
            pltpu.VMEM((mine, width), F32),
            pltpu.VMEM((width // (nx * nz * 2), NW), F32),
            pltpu.VMEM((ny - 1, width, NW), F32),
            dma((5,)),
            dma((2,)),
            dma((2,)),
            dma((2, nz - 1)),
            dma((2, nx - 1)),
            dma((2, nz - 1)),
            dma((2,)),
            dma((2, ny - 1, blocks // ny)),
            dma((2,)),
            dma((2, ny - 1)),
            dma((2, ny - 1, 2)),
            dma((2, ny - 1, 2)),
            dma((2, ny - 1, 2)),
            dma((2, ny - 1, 2)),
            dma((2, ny - 1, nx)),
        ],
        compiler_params=pltpu.CompilerParams(
            collective_id=0, has_side_effects=True, vmem_limit_bytes=62 * 2**20),
        cost_estimate=pl.CostEstimate(
            flops=40_000_000_000, bytes_accessed=30_000_000, transcendentals=1_000_000),
    )(tokens, w_query, w_key, w_value, w_gate, gate_rate.reshape(1, DK), out_grad)

    return mixed, signal


def solution(mesh, shape=(4, 4)):
    nx, nz = shape
    ny = mesh.shape["tp"]
    torus = Mesh(mesh.devices.reshape(nx, nz, 2, ny), SEQ_TP)
    placed = (
        P(SEQ, None),
        P(None, "tp"),
        P(None, "tp"),
        P(None, "tp"),
        P(None, "tp"),
        P("tp"),
        P(SEQ, "tp"),
    )
    return jax.shard_map(
        functools.partial(per_device, (nx, nz, ny)),
        mesh=torus,
        in_specs=placed,
        out_specs=(P(SEQ_TP, None), P(SEQ, "tp")),
        check_vma=False,
    )
```

time: 159 us -> 115 us (0.72)
  Pallas kernels: 126 us -> 110 us
  blocking collectives: 13.7 us -> 0 us
  between operations: 14 us -> 0.65 us
  waiting for transfers between devices: 1.71 us -> 0 us
    pallas_call x1 -> x0, Pallas kernels: 25.4 us -> none  [per_device(): pl.pallas_call(mix_body, grid=(width // tile,), out_shape=jax.ShapeDtypeS...]
    all_gather x1 -> x0, blocking collectives: 13.7 us -> none  [per_device(): gathered = lax.all_gather(piece, 'tp')]
    pallas_call x1, Pallas kernels: 100 us -> 110 us  [per_device(): pl.pallas_call(functools.partial(body, (nx, nz, ny, rows, width, blocks),...]
    unnamed x3 -> x4, local copies, waits for them, and re-layouts: 0.97 us -> 4.46 us
    concatenate x3 -> x0, local copies, waits for them, and re-layouts: 2.26 us -> none  [per_device(): piece = jnp.concatenate(pieces, axis=1).astype(F32)]
    all_gather x1 -> x0, waiting for transfers between devices: 1.69 us -> none  [per_device(): gathered = lax.all_gather(gathered, SEQ, axis=1, tiled=True)]
  transfers between devices with their start and end apart: 1 -> 0, of which waited for: 1 -> 0; matrix products, arithmetic and copies ran while one was open for 0% -> 0% of each run, Pallas kernels for 63% -> 0%
where the time goes in v2:
time: 115 us
  Pallas kernels  110 us (96%)
  local copies, waits for them, and re-layouts  4.46 us (4%)
    pallas_call x1, Pallas kernels, per_device(): pl.pallas_call(functools.partial(body, (nx, nz, ny, rows, width, blocks),...  110 us
    unnamed x4, local copies, waits for them, and re-layouts  4.46 us

profile of v2, /device:TPU:1, one launch (start us, length us, event | category | flops | bytes accessed | tf_op | source)
XLA Modules:
  0.0 115.1 jit_solution(4758422465454558302)
XLA Ops:
  0.6 110.0 %shard_map.86 = (bf16[512,2560]{1,0:T(8,128)(2,1)}, f32[2048,128]{1,0:T(8,128)}) custom-call(bf16[2048,2560]{1,0:T(8,128)(2,1)} %tok_hbm.1, bf16[2560,128]{1,0:T(8,128)(2,1)} %wq.1, bf16[2560,128]{1,0:T(8,128)(2,1)} %wk.1, bf16[2560,256]{1,0:T(8,128)(2,1)} %wv.1, bf16[2560,128]{1,0:T(8,128)(2,1)} %wg.1, f32[1,128]{1,0:T(1,128)} %bitcast.1, ...), custom_call_target="tpu_custom_call" | custom-call | flops 40000000000 | bytes 30000000 | tf_op jit(solution)/shard_map/pallas_call | solution.py:430
  110.6 0.0 copy-start
  110.6 3.5 %copy.11 = bf16[512,2560]{1,0:T(8,128)(2,1)} copy(bf16[512,2560]{1,0:T(8,128)(2,1)} %get-tuple-element.4) | data formatting | bytes 5242880
  114.1 0.0 copy-done
  114.1 1.0 copy.12
Async XLA Ops:
  110.6 3.5 %copy-start = (f32[2048,128]{1,0:T(8,128)S(1)}, f32[2048,128]{1,0:T(8,128)}, u32[]{:S(2)}) copy-start(f32[2048,128]{1,0:T(8,128)} %get-tuple-element.5) | copy-start | bytes 3145732

commit v3 on v2

--- a/solution.py
+++ b/solution.py
@@ -37,11 +37,16 @@
     return high, (a - high.astype(F32)).astype(BF16)
 
 
+def steps(ny):
+    return sorted(range(1, ny), key=lambda o: (-min(o, ny - o), o))
+
+
 def body(dims, signal_scale, tok_hbm, wq, wk, wv, wg, rate_ref, og_hbm, out_hbm, gs_hbm,
          w_s, tok_s, og_s, qt, kt, vs, cs, sq, tri, carry, spre, gpre, dmsg, dpart, zsend, zrecv, zexc,
-         xsend, xrecv, fsend, frecv, psend, states, gbuf, rbuf, gsb, acc, wsend, wl,
-         load_sem, tok_sem, d_sem, z_sem, x_sem, f_sem, p_sem, a_sem, out_sem,
-         wy_sem, w1_sem, f1_sem, w2_sem, f2_sem, wd_sem):
+         xsend, xrecv, fsend, frecv, psend, states, gsb, acc, wsend, wl,
+         low, osend, orecv, ssend, srecv, gsend,
+         load_sem, tok_sem, d_sem, z_sem, x_sem, f_sem, p_sem, out_sem,
+         wy_sem, w1_sem, f1_sem, w2_sem, f2_sem, wd_sem, og_sem, s_sem, gs_sem):
     nx, nz, ny, rows, width, blocks = dims
     x, z, c, y = (lax.axis_index(a) for a in SEQ_TP)
     sgn = 1 - 2 * c
@@ -49,6 +54,8 @@
     quarter = DV // nz
     pairs = blocks // 2
     mine = rows // ny
+    near = steps(ny)
+    order = [o - 1 for o in near]
 
     ring = nx
     share = width // (ring * ring * 2)
@@ -89,9 +96,9 @@
         ref = wl.at[s, share_at(first, wrap(second - 1 + 2 * turn), turn, 2)]
         return remote(ref, ref, f1_sem, (s, turn), place(first, wrap(second + 1 - 2 * turn)))
 
-    def w2_copy(s, turn):
-        ref = wl.at[s, group_at(first, 0, 1)]
-        return remote(ref, ref, w2_sem, (s, turn), place(wrap(first + 1 - 2 * turn), second))
+    def w2_copy(s, turn, half):
+        ref = wl.at[s, group_at(first, half, 2)]
+        return remote(ref, ref, w2_sem, (s, turn, half), place(wrap(first + 1 - 2 * turn), second))
 
     def f2_copy(s, turn):
         ref = wl.at[s, group_at(wrap(first - 1 + 2 * turn), turn, 2)]
@@ -118,22 +125,39 @@
     for peer in peers:
         pl.semaphore_signal(barrier, inc=1, device_id=peer, device_id_type=MESH)
 
-    loads = [
+    weight_loads = [
         pltpu.make_async_copy(wq, w_s.at[:, pl.ds(0, DK)], load_sem.at[0]),
         pltpu.make_async_copy(wk, w_s.at[:, pl.ds(DK, DK)], load_sem.at[1]),
         pltpu.make_async_copy(wv, w_s.at[:, pl.ds(2 * DK, DV)], load_sem.at[2]),
         pltpu.make_async_copy(wg, w_s.at[:, pl.ds(2 * DK + DV, DK)], load_sem.at[3]),
-        pltpu.make_async_copy(og_hbm, og_s, load_sem.at[4]),
     ]
+    grad_load = pltpu.make_async_copy(og_hbm, og_s, load_sem.at[4])
 
     def tok_copy(i):
         slot = lax.rem(i, 2)
         start = pl.multiple_of(i * 2 * BT, 2 * BT)
         return pltpu.make_async_copy(tok_hbm.at[pl.ds(start, 2 * BT)], tok_s.at[slot], tok_sem.at[slot])
 
+    def chunk(j):
+        return pl.ds(pl.multiple_of(j * mine, mine), mine)
+
+    def block_rows(b):
+        return pl.ds(pl.multiple_of(b * BT, BT), BT)
+
+    def og_copy(m, o):
+        return remote(osend.at[m], orecv.at[m], og_sem, (m,), {"tp": lax.rem(y + o, ny)})
+
+    def state_copy(m, o):
+        return remote(ssend.at[m], srecv.at[m], s_sem, (m,), {"tp": lax.rem(y + o, ny)})
+
+    def signal_copy(m, o, i):
+        return remote(gsend.at[m, block_rows(i)], gsb.at[block_rows(y * per_chunk + i)], gs_sem, (m, i),
+                      {"tp": lax.rem(y - o + ny, ny)})
+
+    for load in weight_loads:
+        load.start()
     tok_copy(0).start()
-    for load in loads:
-        load.start()
+    grad_load.start()
 
     at = lax.broadcasted_iota(jnp.int32, (BT, BT), 0)
     before = lax.broadcasted_iota(jnp.int32, (BT, BT), 1)
@@ -143,49 +167,127 @@
     spre[0] = jnp.zeros((DV, DK), F32)
     gpre[0] = jnp.zeros((DV, DK), F32)
     rate = rate_ref[...]
-    for load in loads:
-        load.wait()
+    with jax.named_scope("wload"):
+        for load in weight_loads:
+            load.wait()
     wsend[...] = w_s[share_at(first, second, 0, 1), :].astype(F32)
-    pl.semaphore_wait(barrier, len(peers))
-    for o in range(1, ny):
-        wy_copy(o).start()
+    with jax.named_scope("barrier"):
+        pl.semaphore_wait(barrier, len(peers))
+    for s in order:
+        wy_copy(s + 1).start()
+
+    def absorb(b, qk, val, gate, rate_here, cot_rows):
+        rows_b = block_rows(b)
+        squashed = jax.nn.sigmoid(gate)
+        sq[rows_b, :] = squashed
+        high, low = split(-rate_here * squashed)
+        running = mm(tri[0], high) + mm(tri[0], low) + carry[0:1, :]
+        carry[0:1, :] = running[BT - 1:BT, :]
+        cs[rows_b, :] = running
+        q_here = qk[:, 0:DK].astype(BF16).astype(F32)
+        k_here = qk[:, DK:2 * DK].astype(BF16).astype(F32)
+        q_run = (q_here * jnp.exp(running)).astype(BF16)
+        k_run = (k_here * jnp.exp(-running)).astype(BF16)
+        v_here = val.astype(BF16)
+        qt[rows_b, :] = q_run
+        kt[rows_b, :] = k_run
+        vs[rows_b, :] = v_here
+        spre[b + 1] = spre[b] + mm_tn(v_here, k_run)
+        gpre[b + 1] = gpre[b] + mm_tn(cot_rows, q_run)
+
+    def gradients(b, s_in, g_out, last, rate_here):
+        rows_b = block_rows(b)
+        q_run = qt[rows_b, :]
+        k_run = kt[rows_b, :]
+        v_here = vs[rows_b, :]
+        o_grad = og_s[rows_b, :]
+        running = cs[rows_b, :]
+        squashed = sq[rows_b, :]
+        upper = tri[1].astype(F32)
+        lower = tri[0].astype(F32)
+        scores_t = (mm_nt(k_run, q_run) * upper).astype(BF16)
+        d_scores = (mm_nt(o_grad, v_here) * lower).astype(BF16)
+        d_scores_t = (mm_nt(v_here, o_grad) * upper).astype(BF16)
+        state = s_in + spre[b]
+        after = s_in + spre[b + 1]
+        cotangent = g_out + (gpre[last] - gpre[b + 1])
+        state_low = state.astype(BF16)
+        cot_low = cotangent.astype(BF16)
+        dv = mm(scores_t, o_grad) + mm_nt(k_run, cot_low)
+        dq = mm(o_grad, state_low) + mm(d_scores, k_run)
+        dk = mm(v_here, cot_low) + mm(d_scores_t, q_run)
+        boundary = jnp.sum(after * cotangent, axis=0, keepdims=True)
+        high, low = split(q_run.astype(F32) * dq - k_run.astype(F32) * dk)
+        dg = mm(tri[1], high) + mm(tri[1], low) + boundary
+        pre = dg * (-rate_here) * squashed * (1.0 - squashed)
+        return dq * jnp.exp(running), dk * jnp.exp(-running), dv, pre
+
+    def put(ref, rows_b, parts):
+        dq, dk, dv, pre = parts
+        ref[rows_b, 0:DK] = dq.astype(ref.dtype)
+        ref[rows_b, DK:2 * DK] = dk.astype(ref.dtype)
+        ref[rows_b, 2 * DK:2 * DK + DV] = dv.astype(ref.dtype)
+        ref[rows_b, 2 * DK + DV:] = pre.astype(ref.dtype)
 
     with jax.named_scope("proj"):
         @pl.loop(0, pairs)
         def _(i):
-            slot = lax.rem(i, 2)
-
             @pl.when(i + 1 < pairs)
             def _():
                 tok_copy(i + 1).start()
 
+            @pl.when(i == 0)
+            def _():
+                grad_load.wait()
+
+            @pl.when(i == pairs - 2)
+            def _():
+                for s in order[:2]:
+                    wy_copy(s + 1).wait_recv()
+                    start_all(w1_copy, s)
+
+            @pl.when(i == pairs - 1)
+            def _():
+                for s in order[2:]:
+                    wy_copy(s + 1).wait_recv()
+                    start_all(w1_copy, s)
+                for s in order[:1]:
+                    arrive_all(w1_copy, s)
+                    if ring > 2:
+                        start_all(f1_copy, s)
+
             tok_copy(i).wait()
-            here = tok_s[slot]
+            here = tok_s[lax.rem(i, 2)]
             qk = mm(here, w_s[:, 0:2 * DK])
             val = mm(here, w_s[:, 2 * DK:2 * DK + DV])
             gate = mm(here, w_s[:, 2 * DK + DV:])
             for half in range(2):
                 b = i * 2 + half
-                at_rows = pl.ds(pl.multiple_of(b * BT, BT), BT)
                 part = slice(half * BT, (half + 1) * BT)
-                squashed = jax.nn.sigmoid(gate[part])
-                sq[at_rows, :] = squashed
-                high, low = split(-rate * squashed)
-                running = mm(tri[0], high) + mm(tri[0], low) + carry[0:1, :]
-                carry[0:1, :] = running[BT - 1:BT, :]
-                cs[at_rows, :] = running
-                q_here = qk[part, 0:DK].astype(BF16).astype(F32)
-                k_here = qk[part, DK:2 * DK].astype(BF16).astype(F32)
-                q_run = (q_here * jnp.exp(running)).astype(BF16)
-                k_run = (k_here * jnp.exp(-running)).astype(BF16)
-                v_here = val[part].astype(BF16)
-                qt[at_rows, :] = q_run
-                kt[at_rows, :] = k_run
-                vs[at_rows, :] = v_here
-                spre[b + 1] = spre[b] + mm_tn(v_here, k_run)
-                gpre[b + 1] = gpre[b] + mm_tn(og_s[at_rows, :], q_run)
-
-
+                absorb(b, qk[part], val[part], gate[part], rate, og_s[block_rows(b), :])
+
+    x_chunk = pltpu.make_async_copy(tok_hbm.at[chunk(y)], tok_s.at[0, pl.ds(0, mine)], tok_sem.at[0])
+    x_chunk.start()
+    for s in order[1:]:
+        arrive_all(w1_copy, s)
+        if ring > 2:
+            start_all(f1_copy, s)
+
+    def start_w2(s, halves=(0, 1)):
+        if ring > 2 and 0 in halves:
+            arrive_all(f1_copy, s)
+        for half in halves:
+            for turn in turns:
+                w2_copy(s, turn, half).start()
+
+    def arrive_w2(s):
+        for half in range(2):
+            for turn in turns:
+                w2_copy(s, turn, half).wait_recv()
+
+    @pl.when(c == 0)
+    def _():
+        start_w2(order[0])
     log_total = carry[0:1, :]
     decay = jnp.exp(log_total)
     dmsg[0, 0:DV, :] = spre[blocks] * decay
@@ -213,10 +315,14 @@
             device_id={"seq_1": to}, device_id_type=MESH))
     for copy in z_copies:
         copy.start()
-    slots = [0, 2, 1][: ny - 1] if ny > 2 else [0]
-    for s in range(ny - 1):
-        wy_copy(s + 1).wait_recv()
-    start_all(w1_copy, slots[0])
+    for m, o in enumerate(near):
+        osend[m] = og_s[chunk(lax.rem(y + o, ny)), :].astype(F32)
+    for m, o in enumerate(near):
+        og_copy(m, o).start()
+    @pl.when(c == 1)
+    def _():
+        start_w2(order[0])
+
     with jax.named_scope("zex"):
         for copy in z_copies:
             copy.wait()
@@ -243,8 +349,15 @@
     for d in range(1, nx):
         inside, copy = x_copy(d)
         pl.when(inside)(copy.start)
-    for s in slots[1:2]:
-        start_all(w1_copy, s)
+
+    for s in order[1:2]:
+        start_w2(s, (0,))
+
+    @pl.when(c == 0)
+    def _():
+        for s in order[1:2]:
+            start_w2(s, (1,))
+
     with jax.named_scope("xex"):
         for d in range(1, nx):
             inside, copy = x_copy(d)
@@ -266,8 +379,12 @@
             device_id={"seq_1": to}, device_id_type=MESH))
     for copy in f_copies:
         copy.start()
-    for s in slots[2:]:
-        start_all(w1_copy, s)
+
+    @pl.when(c == 1)
+    def _():
+        for s in order[1:2]:
+            start_w2(s, (1,))
+
     with jax.named_scope("fex"):
         for copy in f_copies:
             copy.wait()
@@ -277,81 +394,51 @@
     states[c] = entered
     p_copy = pltpu.make_async_remote_copy(
         psend, states.at[c], p_sem.at[0], p_sem.at[1], device_id={"seq_2": 1 - c}, device_id_type=MESH)
+    def group_done(s):
+        if ring > 2:
+            start_all(f2_copy, s)
+        for n in sorted({0, 1, ring - 1}):
+            wd_copy(s, n).start()
+
+    def whole(s):
+        if ring > 2:
+            arrive_all(f2_copy, s)
+            wd_copy(s, 2).start()
+        for n in range(ring):
+            wd_copy(s, n).wait_recv()
+
+    p_copy.start()
+    with jax.named_scope("w2z"):
+        arrive_w2(order[0])
+        group_done(order[0])
     with jax.named_scope("pex"):
-        p_copy.start()
         p_copy.wait()
 
     states[1] = states[1] * decay
-    for s in slots:
-        arrive_all(w1_copy, s)
-        if ring > 2:
-            start_all(f1_copy, s)
-
-    def a_copy(n):
-        o = lax.rem(n // per_chunk + 1, ny)
-        i = lax.rem(n, per_chunk)
+    for m, o in enumerate(near):
         to = lax.rem(y + o, ny)
-        b = to * per_chunk + i
-        return o, i, to, b
-
-    def start_send(n):
-        o, i, to, b = a_copy(n)
-        dst = pl.ds(pl.multiple_of(i * BT, BT), BT)
-        slot = o - 1
-        return pltpu.make_async_remote_copy(
-            gbuf.at[b], rbuf.at[slot, dst], a_sem.at[0, slot, i], a_sem.at[1, slot, i],
-            device_id={"tp": to}, device_id_type=MESH)
-
-    sent = blocks - per_chunk
-
-    with jax.named_scope("blk"):
-        @pl.loop(0, blocks)
-        def _(n):
-            o, i, to, b = a_copy(n)
-            at_rows = pl.ds(pl.multiple_of(b * BT, BT), BT)
-            q_run = qt[at_rows, :]
-            k_run = kt[at_rows, :]
-            v_here = vs[at_rows, :]
-            o_grad = og_s[at_rows, :]
-            running = cs[at_rows, :]
-            squashed = sq[at_rows, :]
-            upper = tri[1].astype(F32)
-            lower = tri[0].astype(F32)
-            scores_t = (mm_nt(k_run, q_run) * upper).astype(BF16)
-            d_scores = (mm_nt(o_grad, v_here) * lower).astype(BF16)
-            d_scores_t = (mm_nt(v_here, o_grad) * upper).astype(BF16)
-            state = states[0] + spre[b]
-            after = states[0] + spre[b + 1]
-            cotangent = states[1] + (gpre[blocks] - gpre[b + 1])
-            state_low = state.astype(BF16)
-            cot_low = cotangent.astype(BF16)
-            dv = mm(scores_t, o_grad) + mm_nt(k_run, cot_low)
-            dq = mm(o_grad, state_low) + mm(d_scores, k_run)
-            dk = mm(v_here, cot_low) + mm(d_scores_t, q_run)
-            boundary = jnp.sum(after * cotangent, axis=0, keepdims=True)
-            high, low = split(q_run.astype(F32) * dq - k_run.astype(F32) * dk)
-            dg = mm(tri[1], high) + mm(tri[1], low) + boundary
-            pre = dg * (-rate) * squashed * (1.0 - squashed)
-            gsb[at_rows, :] = pre * signal_scale
-            gbuf[b, :, 0:DK] = dq * jnp.exp(running)
-            gbuf[b, :, DK:2 * DK] = dk * jnp.exp(-running)
-            gbuf[b, :, 2 * DK:2 * DK + DV] = dv
-            gbuf[b, :, 2 * DK + DV:] = pre
-
-            @pl.when((n >= 1) & (n - 1 < sent))
-            def _():
-                start_send(n - 1).start()
-
-            @pl.when(n == 2)
-            def _():
-                for s in slots:
-                    if ring > 2:
-                        arrive_all(f1_copy, s)
-                    start_all(w2_copy, s)
-
-
-    gs_copy = pltpu.make_async_copy(gsb, gs_hbm, out_sem.at[0])
-    gs_copy.start()
+        start_log = cs[pl.ds(pl.multiple_of(jnp.maximum(to * mine - 8, 0), 8), 8), :][7:8, :]
+        start_log = jnp.where(to > 0, start_log, 0.0)
+        ssend[m, 0, 0:DV, :] = (states[0] + spre[to * per_chunk]) * jnp.exp(start_log)
+        ssend[m, 1, 0:DV, :] = (states[1] + (gpre[blocks] - gpre[(to + 1) * per_chunk])) * jnp.exp(-start_log)
+        ssend[m, 0, DV:DV + 8, :] = jnp.broadcast_to(rate, (8, DK))
+        ssend[m, 1, DV:DV + 8, :] = jnp.broadcast_to(rate, (8, DK))
+
+    for m, o in enumerate(near):
+        state_copy(m, o).start()
+
+    with jax.named_scope("own"):
+        for i in range(per_chunk):
+            b = y * per_chunk + i
+            parts = gradients(b, states[0], states[1], blocks, rate)
+            gsb[block_rows(b), :] = parts[3] * signal_scale
+            put(low, block_rows(i), parts)
+    with jax.named_scope("w2a"):
+        for s in order[1:2]:
+            arrive_w2(s)
+            group_done(s)
+        for s in order[2:]:
+            start_w2(s)
     cols = min(512, width)
 
     def mix(grads, weights, last):
@@ -362,57 +449,75 @@
             if last is None:
                 acc[:, at] = term
             elif last:
-                tok_s[0, 0:mine, at] = (acc[:, at] + term).astype(BF16)
+                tok_s[1, 0:mine, at] = (acc[:, at] + term).astype(BF16)
             else:
                 acc[:, at] = acc[:, at] + term
 
+    def fill(s, m):
+        carry[...] = jnp.zeros_like(carry)
+        spre[0] = jnp.zeros((DV, DK), F32)
+        gpre[0] = jnp.zeros((DV, DK), F32)
+        here = tok_s[0, 0:mine, :]
+        qk = mm(here, wl[s, :, 0:2 * DK].astype(BF16))
+        val = mm(here, wl[s, :, 2 * DK:2 * DK + DV].astype(BF16))
+        gate = mm(here, wl[s, :, 2 * DK + DV:].astype(BF16))
+        if m == min(1, len(near) - 1):
+            with jax.named_scope("w2c"):
+                for later in order[2:]:
+                    arrive_w2(later)
+                    group_done(later)
+        with jax.named_scope(f"ogw{m}"):
+            og_copy(m, near[m]).wait_recv()
+        with jax.named_scope(f"stw{m}"):
+            state_copy(m, near[m]).wait_recv()
+        og_s[0:mine, :] = orecv[m].astype(BF16)
+        rate_here = srecv[m, 0, DV:DV + 1, :]
+        for i in range(per_chunk):
+            part = slice(i * BT, (i + 1) * BT)
+            absorb(i, qk[part], val[part], gate[part], rate_here, og_s[block_rows(i), :])
+        for i in range(per_chunk):
+            parts = gradients(i, srecv[m, 0, 0:DV, :], srecv[m, 1, 0:DV, :], per_chunk, rate_here)
+            gsend[m, block_rows(i), :] = parts[3] * signal_scale
+            put(low, block_rows(i), parts)
+            signal_copy(m, near[m], i).start()
+
     with jax.named_scope("mix_own"):
-        own = gbuf[pl.ds(y * per_chunk, per_chunk)].reshape(mine, NW).astype(BF16)
-        mix(own, lambda at: w_s[at, :], None)
-    with jax.named_scope("weights"):
-        for s in slots:
-            for n in range(1):
-                wd_copy(s, n).start()
-        for s in slots:
-            arrive_all(w2_copy, s)
-            if ring > 2:
-                start_all(f2_copy, s)
-            wd_copy(s, 1).start()
-            if ring > 2:
-                wd_copy(s, ring - 1).start()
-        if ring > 2:
-            for s in slots:
-                arrive_all(f2_copy, s)
-                wd_copy(s, 2).start()
-        for s in slots:
+        mix(low[...], lambda at: w_s[at, :], None)
+    x_chunk.wait()
+    for m, o in enumerate(near):
+        s = o - 1
+        with jax.named_scope(f"whole{m}"):
+            whole(s)
+        with jax.named_scope(f"fill{m}"):
+            fill(s, m)
+        with jax.named_scope(f"mix{m}"):
+            mix(low[...], lambda at: wl[s, at, :].astype(BF16), s == order[-1])
+    out_copy = pltpu.make_async_copy(tok_s.at[1, pl.ds(0, mine)], out_hbm, out_sem.at[1])
+    out_copy.start()
+    with jax.named_scope("end"):
+        for m, o in enumerate(near):
+            for i in range(per_chunk):
+                signal_copy(m, o, i).wait_recv()
+        gs_copy = pltpu.make_async_copy(gsb, gs_hbm, out_sem.at[0])
+        gs_copy.start()
+        for s in order:
+            wy_copy(s + 1).wait_send()
+            for turn in turns:
+                w1_copy(s, turn).wait_send()
+                w2_copy(s, turn, 0).wait_send()
+                w2_copy(s, turn, 1).wait_send()
+                if ring > 2:
+                    f1_copy(s, turn).wait_send()
+                    f2_copy(s, turn).wait_send()
             for n in range(ring):
-                wd_copy(s, n).wait_recv()
-    for s in slots:
-        with jax.named_scope("grads"):
+                wd_copy(s, n).wait_send()
+        for m, o in enumerate(near):
+            og_copy(m, o).wait_send()
+            state_copy(m, o).wait_send()
             for i in range(per_chunk):
-                start_send(s * per_chunk + i).wait_recv()
-        with jax.named_scope("mix"):
-            mix(rbuf[s].astype(BF16), lambda at: wl[s, at, :].astype(BF16), s == slots[-1])
-    out_copy = pltpu.make_async_copy(tok_s.at[0, pl.ds(0, mine)], out_hbm, out_sem.at[1])
-    out_copy.start()
-    for o in range(1, ny):
-        wy_copy(o).wait_send()
-    for s in slots:
-        for turn in turns:
-            w1_copy(s, turn).wait_send()
-            w2_copy(s, turn).wait_send()
-            if ring > 2:
-                f1_copy(s, turn).wait_send()
-                f2_copy(s, turn).wait_send()
-        for n in range(ring):
-            wd_copy(s, n).wait_send()
-
-    @pl.loop(0, sent)
-    def _(n):
-        start_send(n).wait_send()
-
-    out_copy.wait()
-    gs_copy.wait()
+                signal_copy(m, o, i).wait_send()
+        out_copy.wait()
+        gs_copy.wait()
 
 
 def per_device(dims, tokens, w_query, w_key, w_value, w_gate, gate_rate, out_grad):
@@ -424,6 +529,7 @@
     whole_tokens = rows * nx * nz * 2
     signal_scale = 4.0 * math.sqrt(whole_tokens * DK / DV)
 
+    count_near = ny - 1
     any_spec = pl.BlockSpec(memory_space=pl.ANY)
     vmem_spec = pl.BlockSpec(memory_space=pltpu.VMEM)
     dma = pltpu.SemaphoreType.DMA
@@ -459,12 +565,16 @@
             pltpu.VMEM((nz, quarter, DK), F32),
             pltpu.VMEM((DV, DK), F32),
             pltpu.VMEM((2, DV, DK), F32),
-            pltpu.VMEM((blocks, BT, NW), F32),
-            pltpu.VMEM((ny - 1, mine, NW), F32),
             pltpu.VMEM((rows, DK), F32),
             pltpu.VMEM((mine, width), F32),
             pltpu.VMEM((width // (nx * nz * 2), NW), F32),
             pltpu.VMEM((ny - 1, width, NW), F32),
+            pltpu.VMEM((mine, NW), BF16),
+            pltpu.VMEM((count_near, mine, DV), F32),
+            pltpu.VMEM((count_near, mine, DV), F32),
+            pltpu.VMEM((count_near, 2, DV + 8, DK), F32),
+            pltpu.VMEM((count_near, 2, DV + 8, DK), F32),
+            pltpu.VMEM((count_near, mine, DK), F32),
             dma((5,)),
             dma((2,)),
             dma((2,)),
@@ -472,14 +582,16 @@
             dma((2, nx - 1)),
             dma((2, nz - 1)),
             dma((2,)),
-            dma((2, ny - 1, blocks // ny)),
             dma((2,)),
             dma((2, ny - 1)),
             dma((2, ny - 1, 2)),
             dma((2, ny - 1, 2)),
-            dma((2, ny - 1, 2)),
+            dma((2, ny - 1, 2, 2)),
             dma((2, ny - 1, 2)),
             dma((2, ny - 1, nx)),
+            dma((2, count_near)),
+            dma((2, count_near)),
+            dma((2, count_near, blocks // ny)),
         ],
         compiler_params=pltpu.CompilerParams(
             collective_id=0, has_side_effects=True, vmem_limit_bytes=62 * 2**20),

time: 115 us -> 102 us (0.89)
  Pallas kernels: 110 us -> 96.3 us
    pallas_call x1, Pallas kernels: 110 us -> 96.3 us  [per_device(): pl.pallas_call(functools.partial(body, (nx, nz, ny, rows, width, blocks),...]
where the time goes in v3:
time: 102 us; the launch traced here: 101 us
  Pallas kernels  96.3 us (94%)
  local copies, waits for them, and re-layouts  4.46 us (4%)
    pallas_call x1, Pallas kernels, per_device(): pl.pallas_call(functools.partial(body, (nx, nz, ny, rows, width, blocks),...  96.3 us
    unnamed x4, local copies, waits for them, and re-layouts  4.46 us

profile of v3, /device:TPU:1, one launch (start us, length us, event | category | flops | bytes accessed | tf_op | source)
XLA Modules:
  0.0 101.4 jit_solution(17799650862273086563)
XLA Ops:
  0.6 96.3 %shard_map.86 = (bf16[512,2560]{1,0:T(8,128)(2,1)}, f32[2048,128]{1,0:T(8,128)}) custom-call(bf16[2048,2560]{1,0:T(8,128)(2,1)} %tok_hbm.1, bf16[2560,128]{1,0:T(8,128)(2,1)} %wq.1, bf16[2560,128]{1,0:T(8,128)(2,1)} %wk.1, bf16[2560,256]{1,0:T(8,128)(2,1)} %wv.1, bf16[2560,128]{1,0:T(8,128)(2,1)} %wg.1, f32[1,128]{1,0:T(1,128)} %bitcast.1, ...), custom_call_target="tpu_custom_call" | custom-call | flops 40000000000 | bytes 30000000 | tf_op jit(solution)/shard_map/pallas_call | solution.py:536
  97.0 0.0 copy-start
  97.0 3.5 %copy.11 = bf16[512,2560]{1,0:T(8,128)(2,1)} copy(bf16[512,2560]{1,0:T(8,128)(2,1)} %get-tuple-element.4) | data formatting | bytes 5242880
  100.5 0.0 copy-done
  100.5 1.0 copy.12
Async XLA Ops:
  97.0 3.5 %copy-start = (f32[2048,128]{1,0:T(8,128)S(1)}, f32[2048,128]{1,0:T(8,128)}, u32[]{:S(2)}) copy-start(f32[2048,128]{1,0:T(8,128)} %get-tuple-element.5) | copy-start | bytes 3145732

commit v4 on v3

--- a/solution.py
+++ b/solution.py
@@ -176,24 +176,35 @@
     for s in order:
         wy_copy(s + 1).start()
 
-    def absorb(b, qk, val, gate, rate_here, cot_rows):
-        rows_b = block_rows(b)
-        squashed = jax.nn.sigmoid(gate)
-        sq[rows_b, :] = squashed
-        high, low = split(-rate_here * squashed)
-        running = mm(tri[0], high) + mm(tri[0], low) + carry[0:1, :]
-        carry[0:1, :] = running[BT - 1:BT, :]
-        cs[rows_b, :] = running
-        q_here = qk[:, 0:DK].astype(BF16).astype(F32)
-        k_here = qk[:, DK:2 * DK].astype(BF16).astype(F32)
-        q_run = (q_here * jnp.exp(running)).astype(BF16)
-        k_run = (k_here * jnp.exp(-running)).astype(BF16)
-        v_here = val.astype(BF16)
-        qt[rows_b, :] = q_run
-        kt[rows_b, :] = k_run
-        vs[rows_b, :] = v_here
-        spre[b + 1] = spre[b] + mm_tn(v_here, k_run)
-        gpre[b + 1] = gpre[b] + mm_tn(cot_rows, q_run)
+    def absorb(first_b, qk, val, gate, rate_here):
+        count = qk.shape[0] // BT
+        parts = [slice(n * BT, (n + 1) * BT) for n in range(count)]
+        squashed = [jax.nn.sigmoid(gate[part]) for part in parts]
+        pieces = [split(-rate_here * part) for part in squashed]
+        running = [mm(tri[0], high) + mm(tri[0], low) for high, low in pieces]
+        base = carry[0:1, :]
+        for n in range(count):
+            running[n] = running[n] + base
+            base = running[n][BT - 1:BT, :]
+        carry[0:1, :] = base
+        q_run = [(qk[parts[n], 0:DK].astype(BF16).astype(F32) * jnp.exp(running[n])).astype(BF16) for n in range(count)]
+        k_run = [(qk[parts[n], DK:2 * DK].astype(BF16).astype(F32) * jnp.exp(-running[n])).astype(BF16)
+                 for n in range(count)]
+        v_here = [val[part].astype(BF16) for part in parts]
+        s_terms = [mm_tn(v_here[n], k_run[n]) for n in range(count)]
+        g_terms = [mm_tn(og_s[block_rows(first_b + n), :], q_run[n]) for n in range(count)]
+        s_sum, g_sum = spre[first_b], gpre[first_b]
+        for n in range(count):
+            rows_b = block_rows(first_b + n)
+            s_sum = s_sum + s_terms[n]
+            g_sum = g_sum + g_terms[n]
+            sq[rows_b, :] = squashed[n]
+            cs[rows_b, :] = running[n]
+            qt[rows_b, :] = q_run[n]
+            kt[rows_b, :] = k_run[n]
+            vs[rows_b, :] = v_here[n]
+            spre[first_b + n + 1] = s_sum
+            gpre[first_b + n + 1] = g_sum
 
     def gradients(b, s_in, g_out, last, rate_here):
         rows_b = block_rows(b)
@@ -261,10 +272,7 @@
             qk = mm(here, w_s[:, 0:2 * DK])
             val = mm(here, w_s[:, 2 * DK:2 * DK + DV])
             gate = mm(here, w_s[:, 2 * DK + DV:])
-            for half in range(2):
-                b = i * 2 + half
-                part = slice(half * BT, (half + 1) * BT)
-                absorb(b, qk[part], val[part], gate[part], rate, og_s[block_rows(b), :])
+            absorb(i * 2, qk, val, gate, rate)
 
     x_chunk = pltpu.make_async_copy(tok_hbm.at[chunk(y)], tok_s.at[0, pl.ds(0, mine)], tok_sem.at[0])
     x_chunk.start()
@@ -285,9 +293,6 @@
             for turn in turns:
                 w2_copy(s, turn, half).wait_recv()
 
-    @pl.when(c == 0)
-    def _():
-        start_w2(order[0])
     log_total = carry[0:1, :]
     decay = jnp.exp(log_total)
     dmsg[0, 0:DV, :] = spre[blocks] * decay
@@ -299,6 +304,7 @@
         dmsg.at[1 - c], dpart, d_sem.at[0], d_sem.at[1], device_id={"seq_2": 1 - c}, device_id_type=MESH)
     with jax.named_scope("d2d"):
         d_copy.start()
+        start_w2(order[0], (0,))
         d_copy.wait()
 
     chip_log = log_total + dpart[DV:DV + 1, :]
@@ -319,9 +325,7 @@
         osend[m] = og_s[chunk(lax.rem(y + o, ny)), :].astype(F32)
     for m, o in enumerate(near):
         og_copy(m, o).start()
-    @pl.when(c == 1)
-    def _():
-        start_w2(order[0])
+    start_w2(order[0], (1,))
 
     with jax.named_scope("zex"):
         for copy in z_copies:
@@ -400,10 +404,12 @@
         for n in sorted({0, 1, ring - 1}):
             wd_copy(s, n).start()
 
-    def whole(s):
+    def last_group(s):
         if ring > 2:
             arrive_all(f2_copy, s)
             wd_copy(s, 2).start()
+
+    def whole(s):
         for n in range(ring):
             wd_copy(s, n).wait_recv()
 
@@ -428,18 +434,17 @@
         state_copy(m, o).start()
 
     with jax.named_scope("own"):
+        made = [gradients(y * per_chunk + i, states[0], states[1], blocks, rate) for i in range(per_chunk)]
         for i in range(per_chunk):
-            b = y * per_chunk + i
-            parts = gradients(b, states[0], states[1], blocks, rate)
-            gsb[block_rows(b), :] = parts[3] * signal_scale
-            put(low, block_rows(i), parts)
+            gsb[block_rows(y * per_chunk + i), :] = made[i][3] * signal_scale
+            put(low, block_rows(i), made[i])
     with jax.named_scope("w2a"):
         for s in order[1:2]:
             arrive_w2(s)
             group_done(s)
         for s in order[2:]:
             start_w2(s)
-    cols = min(512, width)
+    cols = width // 2
 
     def mix(grads, weights, last):
         @pl.loop(0, width // cols)
@@ -472,13 +477,13 @@
             state_copy(m, near[m]).wait_recv()
         og_s[0:mine, :] = orecv[m].astype(BF16)
         rate_here = srecv[m, 0, DV:DV + 1, :]
+        absorb(0, qk, val, gate, rate_here)
+        made = [gradients(i, srecv[m, 0, 0:DV, :], srecv[m, 1, 0:DV, :], per_chunk, rate_here)
+                for i in range(per_chunk)]
         for i in range(per_chunk):
-            part = slice(i * BT, (i + 1) * BT)
-            absorb(i, qk[part], val[part], gate[part], rate_here, og_s[block_rows(i), :])
+            gsend[m, block_rows(i), :] = made[i][3] * signal_scale
+            put(low, block_rows(i), made[i])
         for i in range(per_chunk):
-            parts = gradients(i, srecv[m, 0, 0:DV, :], srecv[m, 1, 0:DV, :], per_chunk, rate_here)
-            gsend[m, block_rows(i), :] = parts[3] * signal_scale
-            put(low, block_rows(i), parts)
             signal_copy(m, near[m], i).start()
 
     with jax.named_scope("mix_own"):
@@ -487,9 +492,14 @@
     for m, o in enumerate(near):
         s = o - 1
         with jax.named_scope(f"whole{m}"):
+            if m != 1:
+                last_group(s)
             whole(s)
         with jax.named_scope(f"fill{m}"):
             fill(s, m)
+        if m == 0:
+            for later in order[1:2]:
+                last_group(later)
         with jax.named_scope(f"mix{m}"):
             mix(low[...], lambda at: wl[s, at, :].astype(BF16), s == order[-1])
     out_copy = pltpu.make_async_copy(tok_s.at[1, pl.ds(0, mine)], out_hbm, out_sem.at[1])

time: 102 us -> 97.9 us (0.960)
  Pallas kernels: 96.3 us -> 92.7 us
    pallas_call x1, Pallas kernels: 96.3 us -> 92.7 us  [per_device(): pl.pallas_call(functools.partial(body, (nx, nz, ny, rows, width, blocks),...]
where the time goes in v4:
time: 97.9 us; the launch traced here: 97.8 us
  Pallas kernels  92.7 us (95%)
  local copies, waits for them, and re-layouts  4.46 us (5%)
    pallas_call x1, Pallas kernels, per_device(): pl.pallas_call(functools.partial(body, (nx, nz, ny, rows, width, blocks),...  92.7 us
    unnamed x4, local copies, waits for them, and re-layouts  4.46 us

profile of v4, /device:TPU:1, one launch (start us, length us, event | category | flops | bytes accessed | tf_op | source)
XLA Modules:
  0.0 97.8 jit_solution(3251504693016187507)
XLA Ops:
  0.6 92.7 %shard_map.86 = (bf16[512,2560]{1,0:T(8,128)(2,1)}, f32[2048,128]{1,0:T(8,128)}) custom-call(bf16[2048,2560]{1,0:T(8,128)(2,1)} %tok_hbm.1, bf16[2560,128]{1,0:T(8,128)(2,1)} %wq.1, bf16[2560,128]{1,0:T(8,128)(2,1)} %wk.1, bf16[2560,256]{1,0:T(8,128)(2,1)} %wv.1, bf16[2560,128]{1,0:T(8,128)(2,1)} %wg.1, f32[1,128]{1,0:T(1,128)} %bitcast.1, ...), custom_call_target="tpu_custom_call" | custom-call | flops 40000000000 | bytes 30000000 | tf_op jit(solution)/shard_map/pallas_call | solution.py:546
  93.3 0.0 copy-start
  93.3 3.5 %copy.11 = bf16[512,2560]{1,0:T(8,128)(2,1)} copy(bf16[512,2560]{1,0:T(8,128)(2,1)} %get-tuple-element.4) | data formatting | bytes 5242880
  96.8 0.0 copy-done
  96.8 1.0 copy.12
Async XLA Ops:
  93.3 3.5 %copy-start = (f32[2048,128]{1,0:T(8,128)S(1)}, f32[2048,128]{1,0:T(8,128)}, u32[]{:S(2)}) copy-start(f32[2048,128]{1,0:T(8,128)} %get-tuple-element.5) | copy-start | bytes 3145732

commit v5 on v4

--- a/solution.py
+++ b/solution.py
@@ -44,9 +44,9 @@
 def body(dims, signal_scale, tok_hbm, wq, wk, wv, wg, rate_ref, og_hbm, out_hbm, gs_hbm,
          w_s, tok_s, og_s, qt, kt, vs, cs, sq, tri, carry, spre, gpre, dmsg, dpart, zsend, zrecv, zexc,
          xsend, xrecv, fsend, frecv, psend, states, gsb, acc, wsend, wl,
-         low, osend, orecv, ssend, srecv, gsend,
+         low, made, fsw, osend, orecv, ssend, srecv, gsend,
          load_sem, tok_sem, d_sem, z_sem, x_sem, f_sem, p_sem, out_sem,
-         wy_sem, w1_sem, f1_sem, w2_sem, f2_sem, wd_sem, og_sem, s_sem, gs_sem):
+         wy_sem, w1_sem, f1_sem, w2_sem, f2_sem, wd_sem, og_sem, s_sem, gs_sem, fy_sem):
     nx, nz, ny, rows, width, blocks = dims
     x, z, c, y = (lax.axis_index(a) for a in SEQ_TP)
     sgn = 1 - 2 * c
@@ -56,6 +56,7 @@
     mine = rows // ny
     near = steps(ny)
     order = [o - 1 for o in near]
+    direct = order[-1] if nx > 2 and ny > 2 else None
 
     ring = nx
     share = width // (ring * ring * 2)
@@ -103,6 +104,10 @@
     def f2_copy(s, turn):
         ref = wl.at[s, group_at(wrap(first - 1 + 2 * turn), turn, 2)]
         return remote(ref, ref, f2_sem, (s, turn), place(wrap(first + 1 - 2 * turn), second))
+
+    def fy_copy():
+        dst = wl.at[direct, group_at(wrap(first + 2), 0, 1)]
+        return remote(fsw, dst, fy_sem, (), {"tp": lax.rem(y + direct + 1, ny)})
 
     def wd_copy(s, n):
         ref = wl.at[s, group_at(lax.rem(first + n, ring), 0, 1)]
@@ -240,43 +245,60 @@
         ref[rows_b, 2 * DK:2 * DK + DV] = dv.astype(ref.dtype)
         ref[rows_b, 2 * DK + DV:] = pre.astype(ref.dtype)
 
+    def project(here, weights):
+        gate = mm(here, weights(2 * DK + DV, NW))
+        return mm(here, weights(0, 2 * DK)), mm(here, weights(2 * DK, 2 * DK + DV)), gate
+
+    def held():
+        return made[:, 0:2 * DK], made[:, 2 * DK:2 * DK + DV], made[:, 2 * DK + DV:]
+
+    def hold(parts):
+        made[:, 0:2 * DK], made[:, 2 * DK:2 * DK + DV], made[:, 2 * DK + DV:] = parts
+
+    def own_weights(first_col, end_col):
+        return w_s[:, first_col:end_col]
+
     with jax.named_scope("proj"):
-        @pl.loop(0, pairs)
+        if pairs > 1:
+            tok_copy(1).start()
+        tok_copy(0).wait()
+        hold(project(tok_s[0], own_weights))
+        grad_load.wait()
+
+        @pl.loop(1, pairs)
         def _(i):
             @pl.when(i + 1 < pairs)
             def _():
                 tok_copy(i + 1).start()
 
-            @pl.when(i == 0)
+            @pl.when(i == pairs - 1)
             def _():
-                grad_load.wait()
-
-            @pl.when(i == pairs - 2)
-            def _():
+                if direct is not None:
+                    fsw[...] = w_s[group_at(wrap(first + 2), 0, 1), :].astype(F32)
+                for m, o in enumerate(near):
+                    osend[m] = og_s[chunk(lax.rem(y + o, ny)), :].astype(F32)
                 for s in order[:2]:
                     wy_copy(s + 1).wait_recv()
                     start_all(w1_copy, s)
-
-            @pl.when(i == pairs - 1)
-            def _():
-                for s in order[2:]:
-                    wy_copy(s + 1).wait_recv()
-                    start_all(w1_copy, s)
-                for s in order[:1]:
-                    arrive_all(w1_copy, s)
-                    if ring > 2:
-                        start_all(f1_copy, s)
+                if direct is not None:
+                    fy_copy().start()
+                for m, o in enumerate(near[:2]):
+                    og_copy(m, o).start()
 
             tok_copy(i).wait()
-            here = tok_s[lax.rem(i, 2)]
-            qk = mm(here, w_s[:, 0:2 * DK])
-            val = mm(here, w_s[:, 2 * DK:2 * DK + DV])
-            gate = mm(here, w_s[:, 2 * DK + DV:])
-            absorb(i * 2, qk, val, gate, rate)
+            parts = project(tok_s[lax.rem(i, 2)], own_weights)
+            absorb(i * 2 - 2, *held(), rate)
+            hold(parts)
+
+        for s in order[2:]:
+            wy_copy(s + 1).wait_recv()
+            start_all(w1_copy, s)
+        absorb(blocks - 2, *held(), rate)
 
     x_chunk = pltpu.make_async_copy(tok_hbm.at[chunk(y)], tok_s.at[0, pl.ds(0, mine)], tok_sem.at[0])
     x_chunk.start()
-    for s in order[1:]:
+
+    def forward_w1(s):
         arrive_all(w1_copy, s)
         if ring > 2:
             start_all(f1_copy, s)
@@ -304,7 +326,8 @@
         dmsg.at[1 - c], dpart, d_sem.at[0], d_sem.at[1], device_id={"seq_2": 1 - c}, device_id_type=MESH)
     with jax.named_scope("d2d"):
         d_copy.start()
-        start_w2(order[0], (0,))
+        for s in order[:2]:
+            forward_w1(s)
         d_copy.wait()
 
     chip_log = log_total + dpart[DV:DV + 1, :]
@@ -321,11 +344,10 @@
             device_id={"seq_1": to}, device_id_type=MESH))
     for copy in z_copies:
         copy.start()
-    for m, o in enumerate(near):
-        osend[m] = og_s[chunk(lax.rem(y + o, ny)), :].astype(F32)
-    for m, o in enumerate(near):
-        og_copy(m, o).start()
-    start_w2(order[0], (1,))
+    with jax.named_scope("w1z"):
+        for s in order[2:]:
+            forward_w1(s)
+        start_w2(order[0])
 
     with jax.named_scope("zex"):
         for copy in z_copies:
@@ -389,34 +411,40 @@
         for s in order[1:2]:
             start_w2(s, (1,))
 
+    def forward_w2(s):
+        arrive_w2(s)
+        if ring > 2 and s != direct:
+            start_all(f2_copy, s)
+
+    def group_done(s):
+        for n in sorted({0, 1, ring - 1}):
+            wd_copy(s, n).start()
+
+    def last_group(s):
+        if ring > 2:
+            if s == direct:
+                fy_copy().wait_recv()
+            else:
+                arrive_all(f2_copy, s)
+            wd_copy(s, 2).start()
+
+    def whole(s):
+        for n in range(ring):
+            wd_copy(s, n).wait_recv()
+
     with jax.named_scope("fex"):
         for copy in f_copies:
             copy.wait()
+    with jax.named_scope("w2z"):
+        forward_w2(order[0])
 
     entered = frecv[...].reshape(DV, DK)
     psend[...] = dmsg[c, 0:DV, :] + decay * entered
     states[c] = entered
     p_copy = pltpu.make_async_remote_copy(
         psend, states.at[c], p_sem.at[0], p_sem.at[1], device_id={"seq_2": 1 - c}, device_id_type=MESH)
-    def group_done(s):
-        if ring > 2:
-            start_all(f2_copy, s)
-        for n in sorted({0, 1, ring - 1}):
-            wd_copy(s, n).start()
-
-    def last_group(s):
-        if ring > 2:
-            arrive_all(f2_copy, s)
-            wd_copy(s, 2).start()
-
-    def whole(s):
-        for n in range(ring):
-            wd_copy(s, n).wait_recv()
-
     p_copy.start()
-    with jax.named_scope("w2z"):
-        arrive_w2(order[0])
-        group_done(order[0])
+    group_done(order[0])
     with jax.named_scope("pex"):
         p_copy.wait()
 
@@ -434,13 +462,13 @@
         state_copy(m, o).start()
 
     with jax.named_scope("own"):
-        made = [gradients(y * per_chunk + i, states[0], states[1], blocks, rate) for i in range(per_chunk)]
+        found = [gradients(y * per_chunk + i, states[0], states[1], blocks, rate) for i in range(per_chunk)]
         for i in range(per_chunk):
-            gsb[block_rows(y * per_chunk + i), :] = made[i][3] * signal_scale
-            put(low, block_rows(i), made[i])
+            gsb[block_rows(y * per_chunk + i), :] = found[i][3] * signal_scale
+            put(low, block_rows(i), found[i])
     with jax.named_scope("w2a"):
         for s in order[1:2]:
-            arrive_w2(s)
+            forward_w2(s)
             group_done(s)
         for s in order[2:]:
             start_w2(s)
@@ -454,7 +482,7 @@
             if last is None:
                 acc[:, at] = term
             elif last:
-                tok_s[1, 0:mine, at] = (acc[:, at] + term).astype(BF16)
+                out_hbm[:, at] = (acc[:, at] + term).astype(BF16)
             else:
                 acc[:, at] = acc[:, at] + term
 
@@ -463,13 +491,11 @@
         spre[0] = jnp.zeros((DV, DK), F32)
         gpre[0] = jnp.zeros((DV, DK), F32)
         here = tok_s[0, 0:mine, :]
-        qk = mm(here, wl[s, :, 0:2 * DK].astype(BF16))
-        val = mm(here, wl[s, :, 2 * DK:2 * DK + DV].astype(BF16))
-        gate = mm(here, wl[s, :, 2 * DK + DV:].astype(BF16))
+        qk, val, gate = project(here, lambda first_col, end_col: wl[s, :, first_col:end_col].astype(BF16))
         if m == min(1, len(near) - 1):
             with jax.named_scope("w2c"):
                 for later in order[2:]:
-                    arrive_w2(later)
+                    forward_w2(later)
                     group_done(later)
         with jax.named_scope(f"ogw{m}"):
             og_copy(m, near[m]).wait_recv()
@@ -478,21 +504,26 @@
         og_s[0:mine, :] = orecv[m].astype(BF16)
         rate_here = srecv[m, 0, DV:DV + 1, :]
         absorb(0, qk, val, gate, rate_here)
-        made = [gradients(i, srecv[m, 0, 0:DV, :], srecv[m, 1, 0:DV, :], per_chunk, rate_here)
+        found = [gradients(i, srecv[m, 0, 0:DV, :], srecv[m, 1, 0:DV, :], per_chunk, rate_here)
                 for i in range(per_chunk)]
         for i in range(per_chunk):
-            gsend[m, block_rows(i), :] = made[i][3] * signal_scale
-            put(low, block_rows(i), made[i])
+            gsend[m, block_rows(i), :] = found[i][3] * signal_scale
+            put(low, block_rows(i), found[i])
         for i in range(per_chunk):
             signal_copy(m, near[m], i).start()
 
     with jax.named_scope("mix_own"):
         mix(low[...], lambda at: w_s[at, :], None)
+    for m, o in enumerate(near):
+        if m >= 2:
+            og_copy(m, o).start()
+    if direct is not None:
+        last_group(direct)
     x_chunk.wait()
     for m, o in enumerate(near):
         s = o - 1
         with jax.named_scope(f"whole{m}"):
-            if m != 1:
+            if m != 1 and s != direct:
                 last_group(s)
             whole(s)
         with jax.named_scope(f"fill{m}"):
@@ -502,14 +533,11 @@
                 last_group(later)
         with jax.named_scope(f"mix{m}"):
             mix(low[...], lambda at: wl[s, at, :].astype(BF16), s == order[-1])
-    out_copy = pltpu.make_async_copy(tok_s.at[1, pl.ds(0, mine)], out_hbm, out_sem.at[1])
-    out_copy.start()
     with jax.named_scope("end"):
         for m, o in enumerate(near):
             for i in range(per_chunk):
                 signal_copy(m, o, i).wait_recv()
-        gs_copy = pltpu.make_async_copy(gsb, gs_hbm, out_sem.at[0])
-        gs_copy.start()
+        gs_hbm[...] = gsb[...]
         for s in order:
             wy_copy(s + 1).wait_send()
             for turn in turns:
@@ -518,16 +546,17 @@
                 w2_copy(s, turn, 1).wait_send()
                 if ring > 2:
                     f1_copy(s, turn).wait_send()
-                    f2_copy(s, turn).wait_send()
+                    if s != direct:
+                        f2_copy(s, turn).wait_send()
             for n in range(ring):
                 wd_copy(s, n).wait_send()
+        if direct is not None:
+            fy_copy().wait_send()
         for m, o in enumerate(near):
             og_copy(m, o).wait_send()
             state_copy(m, o).wait_send()
             for i in range(per_chunk):
                 signal_copy(m, o, i).wait_send()
-        out_copy.wait()
-        gs_copy.wait()
 
 
 def per_device(dims, tokens, w_query, w_key, w_value, w_gate, gate_rate, out_grad):
@@ -546,11 +575,11 @@
     mixed, signal = pl.pallas_call(
         functools.partial(body, (nx, nz, ny, rows, width, blocks), signal_scale),
         out_shape=(
-            jax.ShapeDtypeStruct((mine, width), BF16),
-            jax.ShapeDtypeStruct((rows, DK), F32),
+            pltpu.VMEM((mine, width), BF16),
+            pltpu.VMEM((rows, DK), F32),
         ),
         in_specs=[any_spec] * 5 + [vmem_spec, any_spec],
-        out_specs=(any_spec, any_spec),
+        out_specs=(vmem_spec, vmem_spec),
         scratch_shapes=[
             pltpu.VMEM((width, NW), BF16),
             pltpu.VMEM((2, 2 * BT, width), BF16),
@@ -580,6 +609,8 @@
             pltpu.VMEM((width // (nx * nz * 2), NW), F32),
             pltpu.VMEM((ny - 1, width, NW), F32),
             pltpu.VMEM((mine, NW), BF16),
+            pltpu.VMEM((2 * BT, NW), F32),
+            pltpu.VMEM((width // (2 * nx), NW), F32),
             pltpu.VMEM((count_near, mine, DV), F32),
             pltpu.VMEM((count_near, mine, DV), F32),
             pltpu.VMEM((count_near, 2, DV + 8, DK), F32),
@@ -602,9 +633,10 @@
             dma((2, count_near)),
             dma((2, count_near)),
             dma((2, count_near, blocks // ny)),
+            dma((2,)),
         ],
         compiler_params=pltpu.CompilerParams(
-            collective_id=0, has_side_effects=True, vmem_limit_bytes=62 * 2**20),
+            collective_id=0, has_side_effects=True, vmem_limit_bytes=56 * 2**20),
         cost_estimate=pl.CostEstimate(
             flops=40_000_000_000, bytes_accessed=30_000_000, transcendentals=1_000_000),
     )(tokens, w_query, w_key, w_value, w_gate, gate_rate.reshape(1, DK), out_grad)

time: 97.9 us -> 90.3 us (0.922)
  Pallas kernels: 92.7 us -> 87.1 us
  local copies, waits for them, and re-layouts: 4.46 us -> 2.46 us
    pallas_call x1, Pallas kernels: 92.7 us -> 87.1 us  [per_device(): pl.pallas_call(functools.partial(body, (nx, nz, ny, rows, width, blocks),...]
    unnamed x4 -> x2, local copies, waits for them, and re-layouts: 4.46 us -> 2.46 us
where the time goes in v5:
time: 90.3 us; the launch traced here: 90.2 us
  Pallas kernels  87.1 us (96%)
  local copies, waits for them, and re-layouts  2.46 us (3%)
    pallas_call x1, Pallas kernels, per_device(): pl.pallas_call(functools.partial(body, (nx, nz, ny, rows, width, blocks),...  87.1 us
    unnamed x2, local copies, waits for them, and re-layouts  2.46 us

profile of v5, /device:TPU:1, one launch (start us, length us, event | category | flops | bytes accessed | tf_op | source)
XLA Modules:
  0.0 90.2 jit_solution(5746809739109264782)
XLA Ops:
  0.6 87.1 %shard_map.86 = (bf16[512,2560]{1,0:T(8,128)(2,1)S(1)}, f32[2048,128]{1,0:T(8,128)S(1)}) custom-call(bf16[2048,2560]{1,0:T(8,128)(2,1)} %tok_hbm.1, bf16[2560,128]{1,0:T(8,128)(2,1)} %wq.1, bf16[2560,128]{1,0:T(8,128)(2,1)} %wk.1, bf16[2560,256]{1,0:T(8,128)(2,1)} %wv.1, bf16[2560,128]{1,0:T(8,128)(2,1)} %wg.1, f32[1,128]{1,0:T(1,128)} %bitcast.1, ...), custom_call_target="tpu_custom_call" | custom-call | flops 40000000000 | bytes 30000000 | tf_op jit(solution)/shard_map/pallas_call | solution.py:575
  87.7 1.5 %copy.11 = bf16[512,2560]{1,0:T(8,128)(2,1)} copy(bf16[512,2560]{1,0:T(8,128)(2,1)S(1)} %get-tuple-element.2) | data formatting | bytes 5242880
  89.2 1.0 %copy.12 = f32[2048,128]{1,0:T(8,128)} copy(f32[2048,128]{1,0:T(8,128)S(1)} %get-tuple-element.3) | data formatting | bytes 2097152

commit v6 on v5

--- a/solution.py
+++ b/solution.py
@@ -43,10 +43,10 @@
 
 def body(dims, signal_scale, tok_hbm, wq, wk, wv, wg, rate_ref, og_hbm, out_hbm, gs_hbm,
          w_s, tok_s, og_s, qt, kt, vs, cs, sq, tri, carry, spre, gpre, dmsg, dpart, zsend, zrecv, zexc,
-         xsend, xrecv, fsend, frecv, psend, states, gsb, acc, wsend, wl,
-         low, made, fsw, osend, orecv, ssend, srecv, gsend,
+         xsend, xrecv, fsend, frecv, psend, states, acc, wsend, wl,
+         low, made, fsw, osend, orecv, ssend, srecv,
          load_sem, tok_sem, d_sem, z_sem, x_sem, f_sem, p_sem, out_sem,
-         wy_sem, w1_sem, f1_sem, w2_sem, f2_sem, wd_sem, og_sem, s_sem, gs_sem, fy_sem):
+         wy_sem, w1_sem, f1_sem, w2_sem, f2_sem, wd_sem, og_sem, s_sem, fy_sem):
     nx, nz, ny, rows, width, blocks = dims
     x, z, c, y = (lax.axis_index(a) for a in SEQ_TP)
     sgn = 1 - 2 * c
@@ -154,10 +154,6 @@
 
     def state_copy(m, o):
         return remote(ssend.at[m], srecv.at[m], s_sem, (m,), {"tp": lax.rem(y + o, ny)})
-
-    def signal_copy(m, o, i):
-        return remote(gsend.at[m, block_rows(i)], gsb.at[block_rows(y * per_chunk + i)], gs_sem, (m, i),
-                      {"tp": lax.rem(y - o + ny, ny)})
 
     for load in weight_loads:
         load.start()
@@ -464,14 +460,8 @@
     with jax.named_scope("own"):
         found = [gradients(y * per_chunk + i, states[0], states[1], blocks, rate) for i in range(per_chunk)]
         for i in range(per_chunk):
-            gsb[block_rows(y * per_chunk + i), :] = found[i][3] * signal_scale
+            gs_hbm[block_rows(y * per_chunk + i), :] = found[i][3] * signal_scale
             put(low, block_rows(i), found[i])
-    with jax.named_scope("w2a"):
-        for s in order[1:2]:
-            forward_w2(s)
-            group_done(s)
-        for s in order[2:]:
-            start_w2(s)
     cols = width // 2
 
     def mix(grads, weights, last):
@@ -507,13 +497,28 @@
         found = [gradients(i, srecv[m, 0, 0:DV, :], srecv[m, 1, 0:DV, :], per_chunk, rate_here)
                 for i in range(per_chunk)]
         for i in range(per_chunk):
-            gsend[m, block_rows(i), :] = found[i][3] * signal_scale
             put(low, block_rows(i), found[i])
-        for i in range(per_chunk):
-            signal_copy(m, near[m], i).start()
 
     with jax.named_scope("mix_own"):
         mix(low[...], lambda at: w_s[at, :], None)
+    with jax.named_scope("w2a"):
+        for s in order[1:2]:
+            forward_w2(s)
+            group_done(s)
+        for s in order[2:]:
+            start_w2(s)
+    with jax.named_scope("signals"):
+        @pl.loop(1, ny)
+        def _(n):
+            @pl.when(n == ny - 1)
+            def _():
+                last_group(order[0])
+
+            first_b = lax.rem(y + n, ny) * per_chunk
+            found = [gradients(first_b + i, states[0], states[1], blocks, rate)[3] for i in range(per_chunk)]
+            for i in range(per_chunk):
+                gs_hbm[block_rows(first_b + i), :] = found[i] * signal_scale
+
     for m, o in enumerate(near):
         if m >= 2:
             og_copy(m, o).start()
@@ -523,7 +528,7 @@
     for m, o in enumerate(near):
         s = o - 1
         with jax.named_scope(f"whole{m}"):
-            if m != 1 and s != direct:
+            if m > 1 and s != direct:
                 last_group(s)
             whole(s)
         with jax.named_scope(f"fill{m}"):
@@ -534,10 +539,6 @@
         with jax.named_scope(f"mix{m}"):
             mix(low[...], lambda at: wl[s, at, :].astype(BF16), s == order[-1])
     with jax.named_scope("end"):
-        for m, o in enumerate(near):
-            for i in range(per_chunk):
-                signal_copy(m, o, i).wait_recv()
-        gs_hbm[...] = gsb[...]
         for s in order:
             wy_copy(s + 1).wait_send()
             for turn in turns:
@@ -555,8 +556,6 @@
         for m, o in enumerate(near):
             og_copy(m, o).wait_send()
             state_copy(m, o).wait_send()
-            for i in range(per_chunk):
-                signal_copy(m, o, i).wait_send()
 
 
 def per_device(dims, tokens, w_query, w_key, w_value, w_gate, gate_rate, out_grad):
@@ -604,7 +603,6 @@
             pltpu.VMEM((nz, quarter, DK), F32),
             pltpu.VMEM((DV, DK), F32),
             pltpu.VMEM((2, DV, DK), F32),
-            pltpu.VMEM((rows, DK), F32),
             pltpu.VMEM((mine, width), F32),
             pltpu.VMEM((width // (nx * nz * 2), NW), F32),
             pltpu.VMEM((ny - 1, width, NW), F32),
@@ -615,7 +613,6 @@
             pltpu.VMEM((count_near, mine, DV), F32),
             pltpu.VMEM((count_near, 2, DV + 8, DK), F32),
             pltpu.VMEM((count_near, 2, DV + 8, DK), F32),
-            pltpu.VMEM((count_near, mine, DK), F32),
             dma((5,)),
             dma((2,)),
             dma((2,)),
@@ -632,7 +629,6 @@
             dma((2, ny - 1, nx)),
             dma((2, count_near)),
             dma((2, count_near)),
-            dma((2, count_near, blocks // ny)),
             dma((2,)),
         ],
         compiler_params=pltpu.CompilerParams(

time: 90.3 us -> 85.5 us (0.947)
  Pallas kernels: 87.1 us -> 82.2 us
    pallas_call x1, Pallas kernels: 87.1 us -> 82.2 us  [per_device(): pl.pallas_call(functools.partial(body, (nx, nz, ny, rows, width, blocks),...]
where the time goes in v6:
time: 85.5 us; the launch traced here: 85.3 us
  Pallas kernels  82.2 us (96%)
  local copies, waits for them, and re-layouts  2.46 us (3%)
    pallas_call x1, Pallas kernels, per_device(): pl.pallas_call(functools.partial(body, (nx, nz, ny, rows, width, blocks),...  82.2 us
    unnamed x2, local copies, waits for them, and re-layouts  2.46 us

profile of v6, /device:TPU:1, one launch (start us, length us, event | category | flops | bytes accessed | tf_op | source)
XLA Modules:
  0.0 85.3 jit_solution(13378818168128000605)
XLA Ops:
  0.6 82.2 %shard_map.86 = (bf16[512,2560]{1,0:T(8,128)(2,1)S(1)}, f32[2048,128]{1,0:T(8,128)S(1)}) custom-call(bf16[2048,2560]{1,0:T(8,128)(2,1)} %tok_hbm.1, bf16[2560,128]{1,0:T(8,128)(2,1)} %wq.1, bf16[2560,128]{1,0:T(8,128)(2,1)} %wk.1, bf16[2560,256]{1,0:T(8,128)(2,1)} %wv.1, bf16[2560,128]{1,0:T(8,128)(2,1)} %wg.1, f32[1,128]{1,0:T(1,128)} %bitcast.1, ...), custom_call_target="tpu_custom_call" | custom-call | flops 40000000000 | bytes 30000000 | tf_op jit(solution)/shard_map/pallas_call | solution.py:574
  82.9 1.5 %copy.11 = bf16[512,2560]{1,0:T(8,128)(2,1)} copy(bf16[512,2560]{1,0:T(8,128)(2,1)S(1)} %get-tuple-element.2) | data formatting | bytes 5242880
  84.4 1.0 %copy.12 = f32[2048,128]{1,0:T(8,128)} copy(f32[2048,128]{1,0:T(8,128)S(1)} %get-tuple-element.3) | data formatting | bytes 2097152

commit v7 on v6

--- a/solution.py
+++ b/solution.py
@@ -462,7 +462,7 @@
         for i in range(per_chunk):
             gs_hbm[block_rows(y * per_chunk + i), :] = found[i][3] * signal_scale
             put(low, block_rows(i), found[i])
-    cols = width // 2
+    cols = width
 
     def mix(grads, weights, last):
         @pl.loop(0, width // cols)

time: 85.5 us -> 84.3 us (0.986)
  Pallas kernels: 82.2 us -> 81.1 us
    pallas_call x1, Pallas kernels: 82.2 us -> 81.1 us  [per_device(): pl.pallas_call(functools.partial(body, (nx, nz, ny, rows, width, blocks),...]
where the time goes in v7:
time: 84.3 us; the launch traced here: 84.2 us
  Pallas kernels  81.1 us (96%)
  local copies, waits for them, and re-layouts  2.46 us (3%)
    pallas_call x1, Pallas kernels, per_device(): pl.pallas_call(functools.partial(body, (nx, nz, ny, rows, width, blocks),...  81.1 us
    unnamed x2, local copies, waits for them, and re-layouts  2.46 us

profile of v7, /device:TPU:1, one launch (start us, length us, event | category | flops | bytes accessed | tf_op | source)
XLA Modules:
  0.0 84.2 jit_solution(2424183819411883511)
XLA Ops:
  0.6 81.1 %shard_map.86 = (bf16[512,2560]{1,0:T(8,128)(2,1)S(1)}, f32[2048,128]{1,0:T(8,128)S(1)}) custom-call(bf16[2048,2560]{1,0:T(8,128)(2,1)} %tok_hbm.1, bf16[2560,128]{1,0:T(8,128)(2,1)} %wq.1, bf16[2560,128]{1,0:T(8,128)(2,1)} %wk.1, bf16[2560,256]{1,0:T(8,128)(2,1)} %wv.1, bf16[2560,128]{1,0:T(8,128)(2,1)} %wg.1, f32[1,128]{1,0:T(1,128)} %bitcast.1, ...), custom_call_target="tpu_custom_call" | custom-call | flops 40000000000 | bytes 30000000 | tf_op jit(solution)/shard_map/pallas_call | solution.py:574
  81.8 1.5 %copy.11 = bf16[512,2560]{1,0:T(8,128)(2,1)} copy(bf16[512,2560]{1,0:T(8,128)(2,1)S(1)} %get-tuple-element.2) | data formatting | bytes 5242880
  83.3 1.0 %copy.12 = f32[2048,128]{1,0:T(8,128)} copy(f32[2048,128]{1,0:T(8,128)S(1)} %get-tuple-element.3) | data formatting | bytes 2097152
